TPU v7x, 8 devices: a whole 2x2x1 slice. The times are simulated.
8 devices in a mesh: ep: 4 (over z, y, x), dp: 2 (over core).
Axes of the slice: x: 2, y: 2, z: 1, core: 2. Of those that a mesh axis runs over, the one named last changes fastest.
Arguments:
- tokens: bfloat16 [4096, 768], P(('dp', 'ep'))
- d_out: bfloat16 [4096, 768], P(('dp', 'ep'))
- expert_ids: int32 [2, 4096, 4], P(None, ('dp', 'ep'))
- gate_vals: float32 [2, 4096, 4], P(None, ('dp', 'ep'))
- w_mix: bfloat16 [2, 768, 768], replicated
- w_gate: bfloat16 [2, 16, 768, 1344], P(None, 'ep')
- w_up: bfloat16 [2, 16, 768, 1344], P(None, 'ep')
- w_down: bfloat16 [2, 16, 1344, 768], P(None, 'ep')
Outputs:
- output 1: bfloat16 [4096, 768], P(('dp', 'ep'))
- output 2: bfloat16 [4096, 768], P(('dp', 'ep'))
- output 3: bfloat16 [2, 768, 768], replicated
- output 4: bfloat16 [2, 16, 768, 1344], P(None, 'ep')
- output 5: bfloat16 [2, 16, 768, 1344], P(None, 'ep')
- output 6: bfloat16 [2, 16, 1344, 768], P(None, 'ep')
All inputs are finite; a program needn't handle non-finite values.
Results may differ from a plain program's by a relative error of at most 0.0179635.
Values are sent between devices in bfloat16 or wider.
A program may use at most 1 GiB of HBM per device.

v0:
```python
import jax
import jax.numpy as jnp
from jax import lax
from jax.sharding import PartitionSpec as P

CAP_FACTOR = 3


def silu_parts(pre_gate):
    sig_val = jax.nn.sigmoid(pre_gate)
    return pre_gate * sig_val, sig_val * (1.0 + pre_gate * (1.0 - sig_val))


def route_tables(expert_ids, n_experts, capacity):
    flat_ids = expert_ids.reshape(-1)
    n_copies = flat_ids.shape[0]
    sort_order = jnp.argsort(flat_ids, stable=True)
    counts = jnp.bincount(flat_ids, length=n_experts)
    starts = jnp.cumsum(counts) - counts
    slot_pos = jnp.arange(capacity)
    src_copy = sort_order[jnp.minimum(starts[:, None] + slot_pos[None, :], n_copies - 1)]
    is_valid = slot_pos[None, :] < counts[:, None]
    sorted_ids = flat_ids[sort_order]
    rows_sorted = sorted_ids * capacity + jnp.arange(n_copies) - starts[sorted_ids]
    copy_row = jnp.zeros_like(flat_ids).at[sort_order].set(rows_sorted)
    return src_copy, is_valid, copy_row


def layer_forward(x_in, expert_ids, gate_vals, w_mix, w_gate, w_up, w_down, n_experts, capacity):
    tok_local, d_model = x_in.shape
    top_k = expert_ids.shape[1]
    n_local = w_gate.shape[0]
    mixed = x_in.astype(jnp.float32) + jnp.dot(x_in, w_mix, preferred_element_type=jnp.float32)
    u_act = mixed.astype(jnp.bfloat16)
    src_copy, is_valid, copy_row = route_tables(expert_ids, n_experts, capacity)
    send_buf = jnp.where(is_valid[:, :, None], u_act[src_copy // top_k], 0)
    send_buf = send_buf.reshape(n_experts // n_local, n_local, capacity, d_model)
    recv_buf = lax.all_to_all(send_buf, 'ep', 0, 0, tiled=True)
    pre_gate = jnp.einsum('secd,edf->secf', recv_buf, w_gate, preferred_element_type=jnp.float32)
    pre_up = jnp.einsum('secd,edf->secf', recv_buf, w_up, preferred_element_type=jnp.float32)
    act, _ = silu_parts(pre_gate)
    hidden = (act * pre_up).astype(jnp.bfloat16)
    out_buf = jnp.einsum('secf,efd->secd', hidden, w_down, preferred_element_type=jnp.float32).astype(jnp.bfloat16)
    back_buf = lax.all_to_all(out_buf, 'ep', 0, 0, tiled=True).reshape(n_experts * capacity, d_model)
    out_copy = back_buf[copy_row].reshape(tok_local, top_k, d_model)
    y_out = u_act.astype(jnp.float32) + jnp.sum(gate_vals[:, :, None] * out_copy.astype(jnp.float32), axis=1)
    saved = (x_in, src_copy, is_valid, copy_row, recv_buf, pre_gate, pre_up, hidden)
    return y_out.astype(jnp.bfloat16), saved


def layer_backward(saved, d_y, gate_vals, w_mix, w_gate, w_up, w_down):
    x_in, src_copy, is_valid, copy_row, recv_buf, pre_gate, pre_up, hidden = saved
    tok_local, d_model = d_y.shape
    top_k = gate_vals.shape[1]
    n_experts, capacity = is_valid.shape
    g_dy = (gate_vals[:, :, None] * d_y.astype(jnp.float32)[:, None, :]).astype(jnp.bfloat16)
    g_dy = g_dy.reshape(tok_local * top_k, d_model)
    send_grad = jnp.where(is_valid[:, :, None], g_dy[src_copy], 0).reshape(recv_buf.shape)
    recv_grad = lax.all_to_all(send_grad, 'ep', 0, 0, tiled=True)
    d_hidden = jnp.einsum('secd,efd->secf', recv_grad, w_down, preferred_element_type=jnp.float32)
    act, act_slope = silu_parts(pre_gate)
    d_pre_gate = (d_hidden * pre_up * act_slope).astype(jnp.bfloat16)
    d_pre_up = (d_hidden * act).astype(jnp.bfloat16)
    d_recv = (jnp.einsum('secf,edf->secd', d_pre_gate, w_gate, preferred_element_type=jnp.float32)
              + jnp.einsum('secf,edf->secd', d_pre_up, w_up, preferred_element_type=jnp.float32)).astype(jnp.bfloat16)
    g_gate = jnp.einsum('secd,secf->edf', recv_buf, d_pre_gate, preferred_element_type=jnp.float32).astype(jnp.bfloat16)
    g_up = jnp.einsum('secd,secf->edf', recv_buf, d_pre_up, preferred_element_type=jnp.float32).astype(jnp.bfloat16)
    g_down = jnp.einsum('secf,secd->efd', hidden, recv_grad, preferred_element_type=jnp.float32).astype(jnp.bfloat16)
    g_gate = lax.psum(g_gate, 'dp')
    g_up = lax.psum(g_up, 'dp')
    g_down = lax.psum(g_down, 'dp')
    d_back = lax.all_to_all(d_recv, 'ep', 0, 0, tiled=True).reshape(n_experts * capacity, d_model)
    d_copy = d_back[copy_row].reshape(tok_local, top_k, d_model)
    d_u = (d_y.astype(jnp.float32)
           + jnp.sum(gate_vals[:, :, None] * d_copy.astype(jnp.float32), axis=1)).astype(jnp.bfloat16)
    g_mix = jnp.einsum('td,te->de', x_in, d_u, preferred_element_type=jnp.float32).astype(jnp.bfloat16)
    g_mix = lax.psum(g_mix, ('dp', 'ep'))
    d_x = (d_u.astype(jnp.float32)
           + jnp.einsum('te,de->td', d_u, w_mix, preferred_element_type=jnp.float32)).astype(jnp.bfloat16)
    return d_x, (g_mix, g_gate, g_up, g_down)


def stack_part(grads, index):
    return jnp.stack([entry[index] for entry in grads])


def solution(mesh):
    ep_size = mesh.shape['ep']
    tok_spec = P(('dp', 'ep'), None)
    route_spec = P(None, ('dp', 'ep'), None)
    whole_spec = P(None, None, None)
    expert_spec = P(None, 'ep', None, None)

    def device_step(tokens, d_out, expert_ids, gate_vals, w_mix, w_gate, w_up, w_down):
        n_layers = w_mix.shape[0]
        n_experts = w_gate.shape[1] * ep_size
        tok_local = tokens.shape[0]
        top_k = expert_ids.shape[2]
        capacity = (CAP_FACTOR * tok_local * top_k + n_experts - 1) // n_experts
        layer_in = tokens
        saved_all = []
        for layer in range(n_layers):
            layer_in, saved = layer_forward(layer_in, expert_ids[layer], gate_vals[layer], w_mix[layer],
                                            w_gate[layer], w_up[layer], w_down[layer], n_experts, capacity)
            saved_all.append(saved)
        d_y = d_out
        grads = []
        for layer in reversed(range(n_layers)):
            d_y, grad_set = layer_backward(saved_all[layer], d_y, gate_vals[layer], w_mix[layer],
                                           w_gate[layer], w_up[layer], w_down[layer])
            grads.insert(0, grad_set)
        return (layer_in, d_y, stack_part(grads, 0), stack_part(grads, 1),
                stack_part(grads, 2), stack_part(grads, 3))

    return jax.shard_map(device_step, mesh=mesh,
                         in_specs=(tok_spec, tok_spec, route_spec, route_spec, whole_spec,
                                   expert_spec, expert_spec, expert_spec),
                         out_specs=(tok_spec, tok_spec, whole_spec, expert_spec, expert_spec, expert_spec),
                         check_vma=False)
```

profile of v0, /device:TPU:0, one launch (start us, length us, event | category | flops | bytes accessed | tf_op | source)
XLA Modules:
  0.0 1733.4 jit_solution(11942737039589197679)
XLA Ops:
  8.8 14.7 scatter_custom_fusion
  29.3 34.3 %gather_fusion = s32[6144]{0:T(1024)S(1)} fusion(s32[2048]{0:T(1024)S(1)} %get-tuple-element.8, s32[6144]{0:T(1024)S(1)} %broadcast_clamp_fusion.5), kind=kCustom, calls=%fused_computation | custom fusion | bytes 73728 | tf_op jit(solution)/shard_map/gather | solution.py:21
  66.8 26.1 %gather_fusion.1 = bf16[6144,768]{1,0:T(8,128)(2,1)} fusion(bf16[512,768]{1,0:T(8,128)(2,1)S(1)} %add_convert_fusion.9, s32[6144]{0:T(1024)S(1)} %broadcast_clamp_fusion.1), kind=kCustom, calls=%fused_computation.1 | custom fusion | bytes 18898944 | tf_op jit(solution)/shard_map/gather | solution.py:36
  98.4 109.8 %all_to_all.40 = bf16[4,4,384,768]{3,2,1,0:T(8,128)(2,1)} all-to-all(bf16[4,4,384,768]{3,2,1,0:T(8,128)(2,1)S(1)} %broadcast_select_fusion.3), channel_id=1, replica_groups=mesh['ep'=4,'dp'=2] {'ep'}, dimensions={0} | all-to-all | bytes 18874368 | tf_op jit(solution)/shard_map/all_to_all | solution.py:38
  208.3 25.2 %fusion.40 = f32[4,4,384,1344]{2,3,1,0:T(8,128)} fusion(bf16[4,4,384,768]{3,2,1,0:T(8,128)(2,1)} %all_to_all.40, bf16[2,4,768,1344]{2,3,1,0:T(8,128)(2,1)} %param.13), kind=kOutput, calls=%fused_computation.85 | convolution fusion | flops 12683575296 | bytes 50724864 | tf_op jit(solution)/shard_map/secd,edf->secf/dot_general | solution.py:39
  233.4 34.5 %fusion.12 = (bf16[4,4,384,1344]{2,3,0,1:T(8,128)(2,1)}, f32[4,4,384,1344]{2,3,1,0:T(8,128)}) fusion(f32[4,4,384,1344]{2,3,1,0:T(8,128)} %fusion.40, bf16[2,4,768,1344]{2,3,1,0:T(8,128)(2,1)} %param.14, bf16[4,4,384,768]{3,2,1,0:T(8,128)(2,1)} %all_to_all.40), kind=kOutput, calls=%fused_computation.37 | convolution fusion | flops 12733120512 | bytes 100270080 | tf_op jit(solution)/shard_map/secd,edf->secf/dot_general | solution.py:40
  267.9 22.2 %convert_bitcast_fusion.1 = bf16[4,4,384,768]{3,2,0,1:T(8,128)(2,1)} fusion(bf16[4,4,384,1344]{2,3,0,1:T(8,128)(2,1)} %get-tuple-element.115, bf16[2,4,1344,768]{3,2,1,0:T(8,128)(2,1)} %param.15), kind=kOutput, calls=%fused_computation.68 | convolution fusion | flops 12688293888 | bytes 34209792 | tf_op jit(solution)/shard_map/secf,efd->secd/dot_general | solution.py:43
  290.1 8.3 copy.50
  298.4 5.9 all-to-all-start.1
  304.4 11.8 gather_fusion.2
  317.3 14.8 scatter_custom_fusion.2
  338.5 34.5 %gather_fusion.4 = s32[6144]{0:T(1024)S(1)} fusion(s32[2048]{0:T(1024)S(1)} %get-tuple-element.9, s32[6144]{0:T(1024)S(1)} %broadcast_clamp_fusion.4), kind=kCustom, calls=%fused_computation.4 | custom fusion | bytes 73728 | tf_op jit(solution)/shard_map/gather | solution.py:21
  377.0 7.7 mul.133
  389.9 5.6 select_subtract_fusion.1
  395.5 8.0 scatter_custom_fusion.1
  406.8 26.2 %gather_fusion.8 = bf16[6144,768]{1,0:T(8,128)(2,1)} fusion(bf16[2048,768]{1,0:T(8,128)(2,1)S(1)} %multiply_convert_fusion.1, s32[6144]{0:T(1024)S(1)} %broadcast_clamp_fusion.3), kind=kCustom, calls=%fused_computation.8 | custom fusion | bytes 18898944 | tf_op jit(solution)/shard_map/gather | solution.py:58
  433.1 15.0 gather_fusion.3
  448.1 6.8 reshape.442
  454.8 16.5 multiply_reduce_fusion.3
  474.6 26.1 %gather_fusion.5 = bf16[6144,768]{1,0:T(8,128)(2,1)} fusion(bf16[512,768]{1,0:T(8,128)(2,1)S(1)} %add_convert_fusion.7, s32[6144]{0:T(1024)S(1)} %broadcast_clamp_fusion), kind=kCustom, calls=%fused_computation.5 | custom fusion | bytes 18898944 | tf_op jit(solution)/shard_map/gather | solution.py:36
  500.7 11.6 broadcast_select_fusion.1
  512.3 107.0 %all_to_all.41 = bf16[4,4,384,768]{3,2,1,0:T(8,128)(2,1)} all-to-all(bf16[4,4,384,768]{3,2,1,0:T(8,128)(2,1)S(1)} %get-tuple-element.82), channel_id=1, replica_groups=mesh['ep'=4,'dp'=2] {'ep'}, dimensions={0} | all-to-all | bytes 18874368 | tf_op jit(solution)/shard_map/all_to_all | solution.py:59
  619.4 6.3 all-to-all-start.2
  625.7 25.2 %fusion.32 = f32[4,4,384,1344]{2,3,1,0:T(8,128)} fusion(bf16[4,4,384,768]{3,2,1,0:T(8,128)(2,1)} %all_to_all.41, bf16[2,4,1344,768]{3,2,1,0:T(8,128)(2,1)} %param.15), kind=kOutput, calls=%fused_computation.77 | convolution fusion | flops 12683575296 | bytes 50724864 | tf_op jit(solution)/shard_map/secd,efd->secf/dot_general | solution.py:60
  651.0 76.1 %all-to-all-done.2 = bf16[4,4,384,768]{3,2,1,0:T(8,128)(2,1)} async-done(((bf16[4,4,384,768]{3,2,1,0:T(8,128)(2,1)}), bf16[4,4,384,768]{3,2,1,0:T(8,128)(2,1)}, u32[]{:S(2)}, u32[]{:S(2)}) %all-to-all-start.2) | async-done | bytes 9437216 | tf_op jit(solution)/shard_map/all_to_all | solution.py:38
  727.1 25.2 %fusion.36 = f32[4,4,384,1344]{2,3,1,0:T(8,128)} fusion(bf16[4,4,384,768]{3,2,1,0:T(8,128)(2,1)} %all-to-all-done.2, bf16[2,4,768,1344]{2,3,1,0:T(8,128)(2,1)} %param.13), kind=kOutput, calls=%fused_computation.81 | convolution fusion | flops 12683575296 | bytes 50724864 | tf_op jit(solution)/shard_map/secd,edf->secf/dot_general | solution.py:39
  752.3 52.3 %fusion.6 = (bf16[4,4,384,1344]{2,3,0,1:T(8,128)(2,1)}, bf16[4,4,384,1344]{2,3,0,1:T(8,128)(2,1)}, bf16[4,4,384,1344]{2,3,0,1:T(8,128)(2,1)}) fusion(f32[4,4,384,1344]{2,3,1,0:T(8,128)} %fusion.36, f32[4,4,384,1344]{2,3,1,0:T(8,128)} %fusion.32, bf16[2,4,768,1344]{2,3,1,0:T(8,128)(2,1)} %param.14, bf16[4,4,384,768]{3,2,1,0:T(8,128)(2,1)} %all-to-all-done.2), kind=kOutput, calls=%fused_computation.27 | convolution fusion | flops 12807438336 | bytes 133300224 | tf_op jit(solution)/shard_map/secd,edf->secf/dot_general | solution.py:40
  804.5 22.3 %convert_bitcast_fusion = bf16[4,4,384,768]{3,2,0,1:T(8,128)(2,1)} fusion(bf16[4,4,384,1344]{2,3,0,1:T(8,128)(2,1)} %get-tuple-element.62, bf16[2,4,1344,768]{3,2,1,0:T(8,128)(2,1)} %param.15), kind=kOutput, calls=%fused_computation.67 | convolution fusion | flops 12688293888 | bytes 34209792 | tf_op jit(solution)/shard_map/secf,efd->secd/dot_general | solution.py:43
  826.8 8.1 copy.57
  834.9 5.8 all-to-all-start.3
  840.7 23.0 %fusion.55 = f32[4,4,384,768]{3,2,1,0:T(8,128)} fusion(bf16[4,4,384,1344]{2,3,0,1:T(8,128)(2,1)} %get-tuple-element.64, bf16[2,4,768,1344]{2,3,1,0:T(8,128)(2,1)} %param.14), kind=kOutput, calls=%fused_computation.100 | convolution fusion | flops 12683575296 | bytes 43646976 | tf_op jit(solution)/shard_map/secf,edf->secd/dot_general | solution.py:65
  863.7 23.6 %fusion.26 = bf16[4,4,384,768]{3,2,0,1:T(8,128)(2,1)} fusion(f32[4,4,384,768]{3,2,1,0:T(8,128)} %fusion.55, bf16[4,4,384,1344]{2,3,0,1:T(8,128)(2,1)} %get-tuple-element.63, bf16[2,4,768,1344]{2,3,1,0:T(8,128)(2,1)} %param.13), kind=kOutput, calls=%fused_computation.65 | convolution fusion | flops 12693012480 | bytes 53084160 | tf_op jit(solution)/shard_map/secf,edf->secd/dot_general | solution.py:64
  887.3 8.1 copy.60
  895.4 48.5 %all-to-all-done.3 = bf16[4,4,384,768]{3,2,1,0:T(8,128)(2,1)} async-done(((bf16[4,4,384,768]{3,2,1,0:T(8,128)(2,1)}), bf16[4,4,384,768]{3,2,1,0:T(8,128)(2,1)}, u32[]{:S(2)}, u32[]{:S(2)}) %all-to-all-start.3) | async-done | bytes 9437216 | tf_op jit(solution)/shard_map/all_to_all | solution.py:44
  943.9 5.8 all-to-all-start.5
  949.7 11.8 gather_fusion.6
  972.9 8.0 scatter_custom_fusion.3
  980.9 13.8 gather_fusion.7
  998.3 54.4 %all-to-all-done.5 = bf16[4,4,384,768]{3,2,1,0:T(8,128)(2,1)} async-done(((bf16[4,4,384,768]{3,2,1,0:T(8,128)(2,1)}), bf16[4,4,384,768]{3,2,1,0:T(8,128)(2,1)}, u32[]{:S(2)}, u32[]{:S(2)}) %all-to-all-start.5) | async-done | bytes 9437216 | tf_op jit(solution)/shard_map/all_to_all | solution.py:72
  1052.8 13.4 gather_fusion.9
  1069.7 20.5 %multiply_reduce_fusion.1 = (f32[512,768]{1,0:T(8,128)S(1)}, f32[512,768]{1,0:T(8,128)}) fusion(f32[512,4,768]{2,1,0:T(4,128)} %reshape.444, f32[512,4]{1,0:T(8,128)S(1)} %copy.51, f32[512,4,768]{2,1,0:T(4,128)} %reshape.443), kind=kLoop, calls=%fused_computation.123 | loop fusion | flops 5505024 | bytes 15736832 | tf_op jit(solution)/shard_map/reduce_sum | solution.py:75
  1097.1 7.7 mul.144
  1108.0 26.2 %gather_fusion.10 = bf16[6144,768]{1,0:T(8,128)(2,1)} fusion(bf16[2048,768]{1,0:T(8,128)(2,1)S(1)} %multiply_convert_fusion, s32[6144]{0:T(1024)S(1)} %broadcast_clamp_fusion.2), kind=kCustom, calls=%fused_computation.10 | custom fusion | bytes 18898944 | tf_op jit(solution)/shard_map/gather | solution.py:58
  1134.2 9.2 broadcast_select_fusion.2
  1143.4 6.0 all-to-all-start.6
  1149.4 20.2 %fusion.43 = bf16[1,4,768,1344]{2,3,1,0:T(8,128)(2,1)} fusion(bf16[4,4,384,768]{3,2,1,0:T(8,128)(2,1)} %all-to-all-done.2, bf16[4,4,384,1344]{2,3,0,1:T(8,128)(2,1)} %get-tuple-element.63), kind=kOutput, calls=%fused_computation.88 | convolution fusion | flops 12687704064 | bytes 34209792 | tf_op jit(solution)/shard_map/secd,secf->edf/dot_general | solution.py:66
  1169.6 20.2 %fusion.45 = bf16[1,4,768,1344]{2,3,1,0:T(8,128)(2,1)} fusion(bf16[4,4,384,768]{3,2,1,0:T(8,128)(2,1)} %all-to-all-done.2, bf16[4,4,384,1344]{2,3,0,1:T(8,128)(2,1)} %get-tuple-element.64), kind=kOutput, calls=%fused_computation.90 | convolution fusion | flops 12687704064 | bytes 34209792 | tf_op jit(solution)/shard_map/secd,secf->edf/dot_general | solution.py:67
  1189.8 62.7 %all-to-all-done.6 = bf16[4,4,384,768]{3,2,1,0:T(8,128)(2,1)} async-done(((bf16[4,4,384,768]{3,2,1,0:T(8,128)(2,1)}), bf16[4,4,384,768]{3,2,1,0:T(8,128)(2,1)}, u32[]{:S(2)}, u32[]{:S(2)}) %all-to-all-start.6) | async-done | bytes 9437216 | tf_op jit(solution)/shard_map/all_to_all | solution.py:59
  1252.5 43.3 %fusion.1 = (bf16[4,4,384,1344]{2,3,0,1:T(8,128)(2,1)}, bf16[4,4,384,1344]{2,3,0,1:T(8,128)(2,1)}) fusion(f32[4,4,384,1344]{2,3,1,0:T(8,128)} %get-tuple-element.116, f32[4,4,384,1344]{2,3,1,0:T(8,128)} %fusion.40, bf16[2,4,1344,768]{3,2,1,0:T(8,128)(2,1)} %param.15, bf16[4,4,384,768]{3,2,1,0:T(8,128)(2,1)} %all-to-all-done.6), kind=kOutput, calls=%fused_computation.19 | convolution fusion | flops 12790923264 | bytes 116785152 | tf_op jit(solution)/shard_map/secd,efd->secf/dot_general | solution.py:60
  1295.8 23.2 %fusion.46 = f32[4,4,384,768]{3,2,1,0:T(8,128)} fusion(bf16[4,4,384,1344]{2,3,0,1:T(8,128)(2,1)} %get-tuple-element.61, bf16[2,4,768,1344]{2,3,1,0:T(8,128)(2,1)} %param.14), kind=kOutput, calls=%fused_computation.91 | convolution fusion | flops 12683575296 | bytes 43646976 | tf_op jit(solution)/shard_map/secf,edf->secd/dot_general | solution.py:65
  1319.0 23.6 %fusion.27 = bf16[4,4,384,768]{3,2,0,1:T(8,128)(2,1)} fusion(f32[4,4,384,768]{3,2,1,0:T(8,128)} %fusion.46, bf16[4,4,384,1344]{2,3,0,1:T(8,128)(2,1)} %get-tuple-element.60, bf16[2,4,768,1344]{2,3,1,0:T(8,128)(2,1)} %param.13), kind=kOutput, calls=%fused_computation.66 | convolution fusion | flops 12693012480 | bytes 53084160 | tf_op jit(solution)/shard_map/secf,edf->secd/dot_general | solution.py:64
  1342.5 8.2 copy.63
  1350.8 5.8 all-to-all-start.7
  1356.6 20.9 %fusion.95 = bf16[1,4,1344,768]{3,2,1,0:T(8,128)(2,1)} fusion(bf16[4,4,384,1344]{2,3,0,1:T(8,128)(2,1)} %get-tuple-element.62, bf16[4,4,384,768]{3,2,1,0:T(8,128)(2,1)} %all_to_all.41), kind=kOutput, calls=%fused_computation.128 | convolution fusion | flops 12687704064 | bytes 34209792 | tf_op jit(solution)/shard_map/secf,secd->efd/dot_general | solution.py:68
  1379.4 20.3 %fusion.92 = bf16[1,4,1344,768]{3,2,1,0:T(8,128)(2,1)} fusion(bf16[4,4,384,1344]{2,3,0,1:T(8,128)(2,1)} %get-tuple-element.115, bf16[4,4,384,768]{3,2,1,0:T(8,128)(2,1)} %all-to-all-done.6), kind=kOutput, calls=%fused_computation.127 | convolution fusion | flops 12687704064 | bytes 34209792 | tf_op jit(solution)/shard_map/secf,secd->efd/dot_general | solution.py:68
  1399.7 17.4 %fusion.42 = bf16[1,4,768,1344]{2,3,1,0:T(8,128)(2,1)} fusion(bf16[4,4,384,768]{3,2,1,0:T(8,128)(2,1)S(1)} %bitcast.292, bf16[4,4,384,1344]{2,3,0,1:T(8,128)(2,1)} %get-tuple-element.60), kind=kOutput, calls=%fused_computation.87 | convolution fusion | flops 12687704064 | bytes 34209792 | tf_op jit(solution)/shard_map/secd,secf->edf/dot_general | solution.py:66
  1417.2 42.5 %all-to-all-done.7 = bf16[4,4,384,768]{3,2,1,0:T(8,128)(2,1)} async-done(((bf16[4,4,384,768]{3,2,1,0:T(8,128)(2,1)}), bf16[4,4,384,768]{3,2,1,0:T(8,128)(2,1)}, u32[]{:S(2)}, u32[]{:S(2)}) %all-to-all-start.7) | async-done | bytes 9437216 | tf_op jit(solution)/shard_map/all_to_all | solution.py:72
  1459.6 13.4 gather_fusion.11
  1476.6 16.7 multiply_reduce_fusion
  1496.8 20.6 %fusion.44 = bf16[1,4,768,1344]{2,3,1,0:T(8,128)(2,1)} fusion(bf16[4,4,384,768]{3,2,1,0:T(8,128)(2,1)} %all_to_all.40, bf16[4,4,384,1344]{2,3,0,1:T(8,128)(2,1)} %get-tuple-element.61), kind=kOutput, calls=%fused_computation.89 | convolution fusion | flops 12687704064 | bytes 34209792 | tf_op jit(solution)/shard_map/secd,secf->edf/dot_general | solution.py:67
  1523.1 25.7 %all-reduce.5.cloned.1.call-done = (bf16[1,768,768]{1,2,0:T(8,128)(2,1)}, bf16[1,768,768]{1,2,0:T(8,128)(2,1)}) async-done(((bf16[1,768,768]{1,2,0:T(8,128)(2,1)}, bf16[1,768,768]{1,2,0:T(8,128)(2,1)}), (bf16[1,768,768]{1,2,0:T(8,128)(2,1)}, bf16[1,768,768]{1,2,0:T(8,128)(2,1)})) %all-reduce.5.cloned.1.call-update) | async-done | bytes 2359312 | tf_op jit(solution)/shard_map/psum | solution.py:77
  1553.1 140.9 %all-reduce.7.cloned.1.call-done = (bf16[1,4,768,1344]{2,3,1,0:T(8,128)(2,1)}, bf16[1,4,768,1344]{2,3,1,0:T(8,128)(2,1)}, bf16[1,4,768,1344]{2,3,1,0:T(8,128)(2,...) async-done(((bf16[1,4,768,1344]{2,3,1,0:T(8,128)(2,1)}, bf16[1,4,768,1344]{2,3,1,0:T(8,128)(2,1)}, ...) | async-done | bytes 49545232 | tf_op jit(solution)/shard_map/psum | solution.py:69
  1694.0 16.3 pad_maximum_fusion.2
  1715.3 11.1 pad_maximum_fusion
  (184 shorter events, 91.7 us)
Async XLA Ops:
  8.8 14.8 copy-start.42
  23.8 39.8 %copy-start.30 = (s32[16]{0:T(128)}, s32[16]{0:T(128)S(1)}, u32[]{:S(2)}) copy-start(s32[16]{0:T(128)S(1)} %sub.28) | copy-start | bytes 196
  24.2 39.5 %copy-start.6 = (s32[2048]{0:T(1024)}, s32[2048]{0:T(1024)S(1)}, u32[]{:S(2)}) copy-start(s32[2048]{0:T(1024)S(1)} %reshape_squeeze.6) | copy-start | bytes 24580
  29.3 34.3 %copy-start.2 = (s32[2048]{0:T(1024)}, s32[2048]{0:T(1024)S(1)}, u32[]{:S(2)}) copy-start(s32[2048]{0:T(1024)S(1)} %get-tuple-element.8) | copy-start | bytes 24580
  29.3 35.0 %copy-start.43 = (bf16[2,768,768]{2,1,0:T(8,128)(2,1)S(1)}, bf16[2,768,768]{2,1,0:T(8,128)(2,1)}, u32[]{:S(2)}) copy-start(bf16[2,768,768]{2,1,0:T(8,128)(2,1)} %param.12) | copy-start | bytes 7077892
  64.4 28.5 %copy-start.35 = (pred[4,4,384]{2,1,0:T(4,128)(4,1)}, pred[4,4,384]{2,1,0:T(4,128)(4,1)S(1)}, u32[]{:S(2)}) copy-start(pred[4,4,384]{2,1,0:T(4,128)(4,1)S(1)} %iota_compare_fusion.1) | copy-start | bytes 18436
  66.8 26.1 %copy-start.8 = (bf16[512,768]{1,0:T(8,128)(2,1)}, bf16[512,768]{1,0:T(8,128)(2,1)S(1)}, u32[]{:S(2)}) copy-start(bf16[512,768]{1,0:T(8,128)(2,1)S(1)} %add_convert_fusion.9) | copy-start | bytes 2359300
  298.4 6.0 copy-start.3
  298.4 6.0 copy-start.7
  298.4 17.8 %copy-start.41 = (f32[2,512,4]{1,2,0:T(4,128)S(1)}, f32[2,512,4]{1,2,0:T(4,128)}, u32[]{:S(2)}) copy-start(f32[2,512,4]{1,2,0:T(4,128)} %param.11) | copy-start | bytes 49156
  298.4 18.6 %copy-start.40 = (s32[1,512,4]{1,2,0:T(4,128)S(1)}, s32[1,512,4]{1,2,0:T(4,128)}, u32[]{:S(2)}) copy-start(s32[1,512,4]{1,2,0:T(4,128)} %get-tuple-element.74) | copy-start | bytes 24580
  298.4 34.7 %copy-start.39 = (s32[1,512,4]{1,2,0:T(4,128)S(1)}, s32[1,512,4]{1,2,0:T(4,128)}, u32[]{:S(2)}) copy-start(s32[1,512,4]{1,2,0:T(4,128)} %get-tuple-element.75) | copy-start | bytes 24580
  298.4 134.7 %all-to-all-start.1 = ((bf16[4,4,384,768]{3,2,1,0:T(8,128)(2,1)}), bf16[4,4,384,768]{3,2,1,0:T(8,128)(2,1)}, u32[]{:S(2)}, u32[]{:S(2)}) async-start(bf16[4,4,384,768]{3,2,1,0:T(8,128)(2,1)} %copy.50), calls=%async_computation.1 | async-start | bytes 18874368 | tf_op jit(solution)/shard_map/all_to_all | solution.py:44
  317.0 137.9 %copy-start.26 = (f32[512,4]{1,0:T(8,128)}, f32[512,4]{1,0:T(8,128)S(1)}, u32[]{:S(2)}) copy-start(f32[512,4]{1,0:T(8,128)S(1)} %copy.44) | copy-start | bytes 24580
  332.5 0.5 copy-start.28
  333.4 39.6 %copy-start.4 = (s32[2048]{0:T(1024)}, s32[2048]{0:T(1024)S(1)}, u32[]{:S(2)}) copy-start(s32[2048]{0:T(1024)S(1)} %reshape_squeeze.7) | copy-start | bytes 24580
  338.5 34.5 %copy-start = (s32[2048]{0:T(1024)}, s32[2048]{0:T(1024)S(1)}, u32[]{:S(2)}) copy-start(s32[2048]{0:T(1024)S(1)} %get-tuple-element.9) | copy-start | bytes 24580
  338.5 34.9 %copy-start.23 = (bf16[512,768]{1,0:T(8,128)(2,1)S(1)}, bf16[512,768]{1,0:T(8,128)(2,1)}, u32[]{:S(2)}) copy-start(bf16[512,768]{1,0:T(8,128)(2,1)} %param.9) | copy-start | bytes 2359300
  373.4 11.2 copy-start.31
  433.1 15.0 copy-start.33
  448.1 24.4 %copy-start.9 = (bf16[512,768]{1,0:T(8,128)(2,1)S(1)}, bf16[512,768]{1,0:T(8,128)(2,1)}, u32[]{:S(2)}) copy-start(bf16[512,768]{1,0:T(8,128)(2,1)} %copy-done.8) | copy-start | bytes 2359300
  471.3 1.2 copy-start.17
  474.6 26.1 %copy-start.11 = (bf16[512,768]{1,0:T(8,128)(2,1)}, bf16[512,768]{1,0:T(8,128)(2,1)S(1)}, u32[]{:S(2)}) copy-start(bf16[512,768]{1,0:T(8,128)(2,1)S(1)} %add_convert_fusion.7) | copy-start | bytes 2359300
  619.4 107.7 %all-to-all-start.2 = ((bf16[4,4,384,768]{3,2,1,0:T(8,128)(2,1)}), bf16[4,4,384,768]{3,2,1,0:T(8,128)(2,1)}, u32[]{:S(2)}, u32[]{:S(2)}) async-start(bf16[4,4,384,768]{3,2,1,0:T(8,128)(2,1)} %get-tuple-element.81), calls=%async_computation.2 | async-start | bytes 18874368 | tf_op jit(solution)/shard_map/all_to_all | solution.py:38
  834.9 109.0 %all-to-all-start.3 = ((bf16[4,4,384,768]{3,2,1,0:T(8,128)(2,1)}), bf16[4,4,384,768]{3,2,1,0:T(8,128)(2,1)}, u32[]{:S(2)}, u32[]{:S(2)}) async-start(bf16[4,4,384,768]{3,2,1,0:T(8,128)(2,1)} %copy.57), calls=%async_computation.3 | async-start | bytes 18874368 | tf_op jit(solution)/shard_map/all_to_all | solution.py:44
  895.4 54.3 %copy-start.1 = (s32[2048]{0:T(1024)S(1)}, s32[2048]{0:T(1024)}, u32[]{:S(2)}) copy-start(s32[2048]{0:T(1024)} %copy-done) | copy-start | bytes 24580
  895.4 54.3 %copy-start.5 = (s32[2048]{0:T(1024)S(1)}, s32[2048]{0:T(1024)}, u32[]{:S(2)}) copy-start(s32[2048]{0:T(1024)} %copy-done.4) | copy-start | bytes 24580
  895.4 66.1 %copy-start.38 = (f32[512,4]{0,1:T(4,128)S(1)}, f32[512,4]{0,1:T(4,128)}, u32[]{:S(2)}) copy-start(f32[512,4]{0,1:T(4,128)} %get-tuple-element.71) | copy-start | bytes 24580
  895.4 66.3 %copy-start.37 = (f32[1,512,4]{1,2,0:T(4,128)S(1)}, f32[1,512,4]{1,2,0:T(4,128)}, u32[]{:S(2)}) copy-start(f32[1,512,4]{1,2,0:T(4,128)} %get-tuple-element.69) | copy-start | bytes 24580
  895.4 66.6 %copy-start.32 = (s32[16,384,1]{1,0,2:T(8,128)S(1)}, s32[16,384,1]{1,0,2:T(8,128)}, u32[]{:S(2)}) copy-start(s32[16,384,1]{1,0,2:T(8,128)} %get-tuple-element.65) | copy-start | bytes 73732
  895.4 66.6 %copy-start.29 = (s32[16]{0:T(128)S(1)}, s32[16]{0:T(128)}, u32[]{:S(2)}) copy-start(s32[16]{0:T(128)} %copy-done.28) | copy-start | bytes 196
  943.9 108.9 %all-to-all-start.5 = ((bf16[4,4,384,768]{3,2,1,0:T(8,128)(2,1)}), bf16[4,4,384,768]{3,2,1,0:T(8,128)(2,1)}, u32[]{:S(2)}, u32[]{:S(2)}) async-start(bf16[4,4,384,768]{3,2,1,0:T(8,128)(2,1)} %copy.60), calls=%async_computation.5 | async-start | bytes 18874368 | tf_op jit(solution)/shard_map/all_to_all | solution.py:72
  1069.7 21.7 %copy-start.24 = (bf16[512,768]{1,0:T(8,128)(2,1)S(1)}, bf16[512,768]{1,0:T(8,128)(2,1)}, u32[]{:S(2)}) copy-start(bf16[512,768]{1,0:T(8,128)(2,1)} %param.9) | copy-start | bytes 2359300
  1069.7 21.7 %copy-start.44 = (bf16[2,768,768]{2,1,0:T(8,128)(2,1)S(1)}, bf16[2,768,768]{2,1,0:T(8,128)(2,1)}, u32[]{:S(2)}) copy-start(bf16[2,768,768]{2,1,0:T(8,128)(2,1)} %param.12) | copy-start | bytes 7077892
  1090.2 1.2 copy-start.21
  1092.3 1.1 copy-start.19
  1108.0 26.2 %copy-start.36 = (pred[4,4,384]{2,1,0:T(4,128)(4,1)S(1)}, pred[4,4,384]{2,1,0:T(4,128)(4,1)}, u32[]{:S(2)}) copy-start(pred[4,4,384]{2,1,0:T(4,128)(4,1)} %copy-done.35) | copy-start | bytes 18436
  1143.4 109.1 %all-to-all-start.6 = ((bf16[4,4,384,768]{3,2,1,0:T(8,128)(2,1)}), bf16[4,4,384,768]{3,2,1,0:T(8,128)(2,1)}, u32[]{:S(2)}, u32[]{:S(2)}) async-start(bf16[4,4,384,768]{3,2,1,0:T(8,128)(2,1)} %broadcast_select_fusion.2), calls=%async_computation.6 | async-start | bytes 18874368 | tf_op jit(solution)/shard_map/all_to_all | solution.py:59
  1350.8 108.9 %all-to-all-start.7 = ((bf16[4,4,384,768]{3,2,1,0:T(8,128)(2,1)}), bf16[4,4,384,768]{3,2,1,0:T(8,128)(2,1)}, u32[]{:S(2)}, u32[]{:S(2)}) async-start(bf16[4,4,384,768]{3,2,1,0:T(8,128)(2,1)} %copy.63), calls=%async_computation.7 | async-start | bytes 18874368 | tf_op jit(solution)/shard_map/all_to_all | solution.py:72
  1356.5 21.0 %copy-start.10 = (bf16[512,768]{1,0:T(8,128)(2,1)S(1)}, bf16[512,768]{1,0:T(8,128)(2,1)}, u32[]{:S(2)}) copy-start(bf16[512,768]{1,0:T(8,128)(2,1)} %copy-done.8) | copy-start | bytes 2359300
  1356.6 21.0 %copy-start.18 = (f32[512,768]{1,0:T(8,128)S(1)}, f32[512,768]{1,0:T(8,128)}, u32[]{:S(2)}) copy-start(f32[512,768]{1,0:T(8,128)} %copy-done.17) | copy-start | bytes 4718596
  1356.6 20.9 %copy-start.25 = (bf16[512,768]{1,0:T(8,128)(2,1)S(1)}, bf16[512,768]{1,0:T(8,128)(2,1)}, u32[]{:S(2)}) copy-start(bf16[512,768]{1,0:T(8,128)(2,1)} %param.9) | copy-start | bytes 2359300
  1356.6 192.2 %all-reduce.5.cloned.1.call-start = ((), (), s32[]{:S(2)}) async-start(), calls=%async_computation.8 | async-start | bytes 4718592 | tf_op jit(solution)/shard_map/psum | solution.py:77
  1356.6 20.9 %copy-start.22 = (f32[512,768]{1,0:T(8,128)S(1)}, f32[512,768]{1,0:T(8,128)}, u32[]{:S(2)}) copy-start(f32[512,768]{1,0:T(8,128)} %copy-done.21) | copy-start | bytes 4718596
  1377.5 22.2 %slice-start = ((s8[9437184]{0:T(1024)(128)(4,1)}), s8[4194304]{0:T(1024)(128)(4,1)S(1)}, s32[]{:S(2)}) async-start(s8[9437184]{0:T(1024)(128)(4,1)} %bitcast.291), calls=%async_computation.10 | async-start | bytes 8388608
  1379.4 20.3 %slice-start.1 = ((s8[9437184]{0:T(1024)(128)(4,1)}), s8[4194304]{0:T(1024)(128)(4,1)S(1)}, s32[]{:S(2)}) async-start(s8[9437184]{0:T(1024)(128)(4,1)} %bitcast.291), calls=%async_computation.11 | async-start | bytes 8388608
  1379.4 20.3 %slice-start.2 = ((s8[9437184]{0:T(1024)(128)(4,1)}), s8[1048576]{0:T(1024)(128)(4,1)S(1)}, s32[]{:S(2)}) async-start(s8[9437184]{0:T(1024)(128)(4,1)} %bitcast.291), calls=%async_computation.12 | async-start | bytes 2097152
  1399.7 59.9 %copy-start.34 = (s32[2048]{0:T(1024)S(1)}, s32[2048]{0:T(1024)}, u32[]{:S(2)}) copy-start(s32[2048]{0:T(1024)} %copy-done.33) | copy-start | bytes 24580
  1473.0 3.6 copy-start.27
  1476.6 18.3 %copy-start.45 = (bf16[512,768]{1,0:T(8,128)(2,1)S(1)}, bf16[512,768]{1,0:T(8,128)(2,1)}, u32[]{:S(2)}) copy-start(bf16[512,768]{1,0:T(8,128)(2,1)} %param.8) | copy-start | bytes 2359300
  1496.7 197.2 %all-reduce.7.cloned.1.call-start = ((), (), s32[]{:S(2)}) async-start(), calls=%async_computation.9 | async-start | bytes 99090432 | tf_op jit(solution)/shard_map/psum | solution.py:69
  1517.4 1.1 copy-start.12
  1517.4 1.7 copy-start.20
  1694.0 16.3 copy-start.13
  1694.0 16.3 copy-start.14
  1694.0 19.0 %copy-start.15 = (bf16[1,4,768,1344]{2,3,1,0:T(8,128)(2,1)S(1)}, bf16[1,4,768,1344]{2,3,1,0:T(8,128)(2,1)}, u32[]{:S(2)}) copy-start(bf16[1,4,768,1344]{2,3,1,0:T(8,128)(2,1)} %get-tuple-element.52) | copy-start | bytes 24772612
  1694.0 21.3 %copy-start.16 = (bf16[1,4,768,1344]{2,3,1,0:T(8,128)(2,1)S(1)}, bf16[1,4,768,1344]{2,3,1,0:T(8,128)(2,1)}, u32[]{:S(2)}) copy-start(bf16[1,4,768,1344]{2,3,1,0:T(8,128)(2,1)} %get-tuple-element.53) | copy-start | bytes 24772612
Sparse Core Ops, SparseCore 0:
  1496.8 51.9 all-reduce.4
  1552.5 141.4 all-reduce.6
where the time goes:
time: 1740 us; the launch traced here: 1730 us
  matrix products  475 us (27%)
  waiting for transfers between devices  451 us (26%)
  local copies, waits for them, and re-layouts  359 us (21%)
  blocking collectives  217 us (12%)
  other arithmetic  181 us (10%)
  starting transfers between devices  35.7 us (2%)
    psum x1, waiting for transfers between devices, layer_backward(): g_gate = lax.psum(g_gate, 'dp')  141 us
    all_to_all x1, blocking collectives, layer_forward(): recv_buf = lax.all_to_all(send_buf, 'ep', 0, 0, tiled=True)  110 us
    all_to_all x1, blocking collectives, layer_backward(): recv_grad = lax.all_to_all(send_grad, 'ep', 0, 0, tiled=True)  107 us
    all_to_all x2, waiting for transfers between devices, layer_backward(): lax.all_to_all(d_recv, 'ep', 0, 0, tiled=True)  96.9 us
    dot_general x2, matrix products, layer_forward(): jnp.einsum('secd,edf->secf', recv_buf, w_up, preferred_element_type=jnp.f...  86.7 us
    all_to_all x1, waiting for transfers between devices, layer_forward(): recv_buf = lax.all_to_all(send_buf, 'ep', 0, 0, tiled=True)  76.1 us
    gather x4, local copies, waits for them, and re-layouts, route_tables(): sort_order[jnp.minimum(starts[:, None] + slot_pos[None, :], n_copies - 1)]  68.8 us
    dot_general x2, matrix products, layer_backward(): jnp.einsum('secd,efd->secf', recv_grad, w_down, preferred_element_type=jn...  68.5 us
  transfers between devices with their start and end apart: 8, of which 7 were waited for; matrix products, arithmetic and copies ran while one was open for 22% of the time, Pallas kernels for 0%

commit v1 on v0

v1 whole, which is shorter than its diff:
```python
import functools

import jax
import jax.numpy as jnp
from jax import lax
from jax.experimental import pallas as pl
from jax.experimental.pallas import tpu as pltpu
from jax.sharding import PartitionSpec as P


TILE = 384
SUB = 128
ALIGN = 16
F_CHUNK = 512
SOURCES = 4
VMEM_LIMIT = 62 * 1024 * 1024
BF16 = jnp.bfloat16
F32 = jnp.float32


def silu_parts(pre_gate):
    sig_val = jax.nn.sigmoid(pre_gate)
    return pre_gate * sig_val, sig_val * (1.0 + pre_gate * (1.0 - sig_val))


def dot_nn(lhs, rhs):
    return lax.dot_general(lhs, rhs, (((1,), (0,)), ((), ())), preferred_element_type=F32)


def dot_nt(lhs, rhs):
    return lax.dot_general(lhs, rhs, (((1,), (1,)), ((), ())), preferred_element_type=F32)


def dot_tn(lhs, rhs):
    return lax.dot_general(lhs, rhs, (((0,), (0,)), ((), ())), preferred_element_type=F32)


def f_chunks(width):
    return [slice(lo, min(lo + F_CHUNK, width)) for lo in range(0, width, F_CHUNK)]


def tile_span(tile):
    return pl.ds(pl.multiple_of(tile * TILE, TILE), TILE)


def row_offsets(count_ref, expert):
    counts = [count_ref[expert, src] for src in range(SOURCES)]
    offsets = [jnp.int32(0)]
    for count in counts:
        offsets.append(offsets[-1] + (count + ALIGN - 1) // ALIGN * ALIGN)
    total = offsets.pop()
    return counts, offsets, jnp.maximum((total + TILE - 1) // TILE, 1)


def per_source(counts, run, capacity):
    small = functools.reduce(jnp.maximum, counts) <= SUB

    @pl.when(small)
    def _():
        for src in range(SOURCES):
            run(src, SUB)

    @pl.when(jnp.logical_not(small))
    def _():
        for src in range(SOURCES):
            pl.when(counts[src] <= SUB)(functools.partial(run, src, SUB))
            pl.when(counts[src] > SUB)(functools.partial(run, src, capacity))


def fetch(pieces, buf, sems, base):
    copies, row = [], 0
    for index, piece in enumerate(pieces):
        rows = piece.shape[0]
        copies.append(pltpu.make_async_copy(piece, buf.at[pl.ds(row, rows)], sems.at[base + index]))
        row += rows
    return copies


def gather(counts, offsets, rank_ref, capacity, tok, write):
    def run(src, rows):
        want = lax.broadcasted_iota(jnp.int32, (rows, tok), 0)
        hot = (rank_ref[0, src:src + 1, :] == want).astype(F32)
        write(src, hot, pl.ds(pl.multiple_of(offsets[src], ALIGN), rows))

    per_source(counts, run, capacity)


def combine(counts, offsets, rank_t_ref, gate_t_ref, buf, acc, capacity, tok):
    def run(src, rows):
        want = lax.broadcasted_iota(jnp.int32, (tok, rows), 1)
        pick = (rank_t_ref[0, :, src:src + 1] == want).astype(BF16)
        values = buf[pl.ds(pl.multiple_of(offsets[src], ALIGN), rows), :]
        span = slice(src * tok, (src + 1) * tok)
        acc[span, :] += gate_t_ref[0, :, src:src + 1] * dot_nn(pick, values)

    per_source(counts, run, capacity)


def put_out(acc, out_refs):
    row = 0
    for out in out_refs:
        rows = out.shape[0]
        out[...] = acc[row:row + rows, :].astype(BF16)
        row += rows


def forward_kernel(n_in, n_out, capacity, *refs):
    count_ref, refs = refs[0], refs[1:]
    u_pieces, refs = refs[:n_in], refs[n_in:]
    rank_ref, rank_t_ref, gate_t_ref, wg_ref, wu_ref, wd_ref = refs[:6]
    outs, refs = refs[6:6 + n_out], refs[6 + n_out:]
    u_buf, x_buf, o_buf, h_buf, acc, sems = refs
    expert = pl.program_id(0)
    tok = rank_t_ref.shape[1]

    @pl.when(expert == 0)
    def _():
        copies = fetch(u_pieces, u_buf, sems, 0)
        for copy in copies:
            copy.start()
        acc[...] = jnp.zeros_like(acc)
        o_buf[...] = jnp.zeros_like(o_buf)
        for copy in copies:
            copy.wait()

    counts, offsets, tiles = row_offsets(count_ref, expert)
    x_buf[tile_span(tiles - 1), :] = jnp.zeros((TILE, x_buf.shape[1]), BF16)

    def write(src, hot, span):
        x_buf[span, :] = dot_nn(hot.astype(BF16), u_buf[src * tok:(src + 1) * tok, :]).astype(BF16)

    gather(counts, offsets, rank_ref, capacity, tok, write)

    def tile_step(tile, carry):
        rows = x_buf[tile_span(tile), :]
        for cols in f_chunks(h_buf.shape[1]):
            pre_gate = dot_nt(rows, wg_ref[0, 0, cols, :])
            pre_up = dot_nt(rows, wu_ref[0, 0, cols, :])
            act, _ = silu_parts(pre_gate)
            h_buf[:, cols] = (act * pre_up).astype(BF16)
        o_buf[tile_span(tile), :] = dot_nn(h_buf[...], wd_ref[0, 0]).astype(BF16)
        return carry

    lax.fori_loop(0, tiles, tile_step, 0)

    combine(counts, offsets, rank_t_ref, gate_t_ref, o_buf, acc, capacity, tok)

    @pl.when(expert == pl.num_programs(0) - 1)
    def _():
        put_out(acc, outs)


def input_grad_kernel(n_u, n_dy, n_out, capacity, *refs):
    count_ref, refs = refs[0], refs[1:]
    u_pieces, refs = refs[:n_u], refs[n_u:]
    dy_pieces, refs = refs[:n_dy], refs[n_dy:]
    rank_ref, gate_ref, rank_t_ref, gate_t_ref, wg_ref, wu_ref, wd_ref = refs[:7]
    outs, refs = refs[7:7 + n_out], refs[7 + n_out:]
    kept, refs = refs[:5], refs[5:]
    u_buf, dy_buf, x_buf, c_buf, v_buf, h_buf, da_buf, db_buf, acc, sems, keep_sems = refs
    expert = pl.program_id(0)
    tok = rank_t_ref.shape[1]

    @pl.when(expert == 0)
    def _():
        copies = fetch(u_pieces, u_buf, sems, 0) + fetch(dy_pieces, dy_buf, sems, n_u)
        for copy in copies:
            copy.start()
        acc[...] = jnp.zeros_like(acc)
        v_buf[...] = jnp.zeros_like(v_buf)
        for copy in copies:
            copy.wait()

    counts, offsets, tiles = row_offsets(count_ref, expert)
    x_buf[tile_span(tiles - 1), :] = jnp.zeros((TILE, x_buf.shape[1]), BF16)
    c_buf[tile_span(tiles - 1), :] = jnp.zeros((TILE, c_buf.shape[1]), BF16)

    def write(src, hot, span):
        pick = hot.astype(BF16)
        toks = slice(src * tok, (src + 1) * tok)
        gate = jnp.sum(hot * gate_ref[0, src:src + 1, :], axis=1, keepdims=True)
        x_buf[span, :] = dot_nn(pick, u_buf[toks, :]).astype(BF16)
        c_buf[span, :] = (gate * dot_nn(pick, dy_buf[toks, :])).astype(BF16)

    gather(counts, offsets, rank_ref, capacity, tok, write)

    def tile_step(tile, carry):
        span = tile_span(tile)
        keep = [pltpu.make_async_copy(src, dst.at[expert, span], keep_sems.at[i]) for i, (src, dst) in enumerate(
            zip((x_buf.at[span], c_buf.at[span], h_buf, da_buf, db_buf), kept))]
        keep[0].start()
        keep[1].start()
        rows = x_buf[span, :]
        grads = c_buf[span, :]
        for cols in f_chunks(h_buf.shape[1]):
            pre_gate = dot_nt(rows, wg_ref[0, 0, cols, :])
            pre_up = dot_nt(rows, wu_ref[0, 0, cols, :])
            d_hid = dot_nt(grads, wd_ref[0, 0, cols, :])
            act, slope = silu_parts(pre_gate)
            h_buf[:, cols] = (act * pre_up).astype(BF16)
            da_buf[:, cols] = (d_hid * pre_up * slope).astype(BF16)
            db_buf[:, cols] = (d_hid * act).astype(BF16)
        for copy in keep[2:]:
            copy.start()
        v_buf[span, :] = (dot_nn(da_buf[...], wg_ref[0, 0]) + dot_nn(db_buf[...], wu_ref[0, 0])).astype(BF16)
        for copy in keep:
            copy.wait()
        return carry

    lax.fori_loop(0, tiles, tile_step, 0)

    combine(counts, offsets, rank_t_ref, gate_t_ref, v_buf, acc, capacity, tok)

    @pl.when(expert == pl.num_programs(0) - 1)
    def _():
        put_out(acc, outs)


def weight_grad_kernel(first, count_ref, x_hbm, c_hbm, h_hbm, da_hbm, db_hbm, out_ref,
                       x_buf, c_buf, h_buf, da_buf, db_buf, acc, slot_ref, sems):
    step = pl.program_id(0)
    n_step = pl.num_programs(0)
    expert = step + first
    tiles = row_offsets(count_ref, expert)[2]

    def copies(which, tile, slot):
        return [pltpu.make_async_copy(src.at[which, tile_span(tile)], dst.at[slot], sems.at[slot, i])
                for i, (src, dst) in enumerate(((x_hbm, x_buf), (c_hbm, c_buf), (h_hbm, h_buf),
                                                (da_hbm, da_buf), (db_hbm, db_buf)))]

    @pl.when(step == 0)
    def _():
        slot_ref[0] = 0
        for copy in copies(expert, 0, 0):
            copy.start()

    def tile_step(tile, slot):
        for copy in copies(expert, tile, slot):
            copy.wait()
        after = 1 - slot

        @pl.when(tile + 1 < tiles)
        def _():
            for copy in copies(expert, tile + 1, after):
                copy.start()

        @pl.when(jnp.logical_and(tile + 1 == tiles, step + 1 < n_step))
        def _():
            for copy in copies(expert + 1, 0, after):
                copy.start()

        begin = tile == 0
        for cols in f_chunks(h_buf.shape[2]):
            acc[0, cols, :] = jnp.where(begin, 0.0, acc[0, cols, :]) + dot_tn(da_buf[slot, :, cols], x_buf[slot])
            acc[1, cols, :] = jnp.where(begin, 0.0, acc[1, cols, :]) + dot_tn(db_buf[slot, :, cols], x_buf[slot])
            acc[2, cols, :] = jnp.where(begin, 0.0, acc[2, cols, :]) + dot_tn(h_buf[slot, :, cols], c_buf[slot])
        return after

    slot_ref[0] = lax.fori_loop(0, tiles, tile_step, slot_ref[0])
    out_ref[0] = acc[...].astype(BF16)


def grad_sum_kernel(own_ref, other_ref, *refs):
    outs = refs[-3:]
    for kind, out in enumerate(outs):
        out[0, 0] = (own_ref[0, kind].astype(F32) + other_ref[0, kind].astype(F32)).astype(BF16)


ANY = pl.BlockSpec(memory_space=pl.ANY)
VMEM = pl.BlockSpec(memory_space=pltpu.VMEM)


def per_expert(shape):
    rest = (0,) * (len(shape) - 1)
    return pl.BlockSpec((1,) + tuple(shape[1:]), lambda e, *_: (e,) + rest)


def layer_weight(layer, shape):
    return pl.BlockSpec((1, 1) + tuple(shape[2:]), lambda e, *_: (layer, e, 0, 0))


def sizes(tables, weights):
    tok = tables[1].shape[2]
    capacity = tok * 3 // 4
    rows_max = (SOURCES * capacity + TILE - 1) // TILE * TILE
    _, n_local, width, d_model = weights[0].shape
    return tok, capacity, rows_max, n_local, width, d_model


def cost(n_dots, d_model, width, n_bytes):
    return pl.CostEstimate(flops=n_dots * 2 * 5 * TILE * d_model * width * 3, bytes_accessed=n_bytes, transcendentals=0)


def expert_forward(layer, u_pieces, tables, weights, out_rows):
    tok, capacity, rows_max, n_local, width, d_model = sizes(tables, weights)
    counts, rank, _, rank_t, gate_t = tables
    n_in, n_out = len(u_pieces), len(out_rows)
    return pl.pallas_call(
        functools.partial(forward_kernel, n_in, n_out, capacity),
        out_shape=[jax.ShapeDtypeStruct((rows, d_model), BF16) for rows in out_rows],
        grid_spec=pltpu.PrefetchScalarGridSpec(
            num_scalar_prefetch=1,
            grid=(n_local,),
            in_specs=[ANY] * n_in + [per_expert(t.shape) for t in (rank, rank_t, gate_t)]
            + [layer_weight(layer, w.shape) for w in weights],
            out_specs=[VMEM] * n_out,
            scratch_shapes=[pltpu.VMEM((SOURCES * tok, d_model), BF16),
                            pltpu.VMEM((rows_max + SUB, d_model), BF16),
                            pltpu.VMEM((rows_max + SUB, d_model), BF16),
                            pltpu.VMEM((TILE, width), BF16),
                            pltpu.VMEM((SOURCES * tok, d_model), F32),
                            pltpu.SemaphoreType.DMA((n_in,))]),
        compiler_params=pltpu.CompilerParams(vmem_limit_bytes=VMEM_LIMIT),
        cost_estimate=cost(3, d_model, width, 3 * 2 * n_local * d_model * width),
        name='expert_forward',
    )(counts, *u_pieces, rank, rank_t, gate_t, *weights)


def expert_input_grad(layer, u_pieces, dy_pieces, tables, weights, out_rows):
    tok, capacity, rows_max, n_local, width, d_model = sizes(tables, weights)
    counts, rank, gate, rank_t, gate_t = tables
    n_u, n_dy, n_out = len(u_pieces), len(dy_pieces), len(out_rows)
    kept = [jax.ShapeDtypeStruct((n_local, rows_max, cols), BF16) for cols in (d_model, d_model, width, width, width)]
    out = pl.pallas_call(
        functools.partial(input_grad_kernel, n_u, n_dy, n_out, capacity),
        out_shape=[jax.ShapeDtypeStruct((rows, d_model), BF16) for rows in out_rows] + kept,
        grid_spec=pltpu.PrefetchScalarGridSpec(
            num_scalar_prefetch=1,
            grid=(n_local,),
            in_specs=[ANY] * (n_u + n_dy) + [per_expert(t.shape) for t in (rank, gate, rank_t, gate_t)]
            + [layer_weight(layer, w.shape) for w in weights],
            out_specs=[VMEM] * n_out + [ANY] * 5,
            scratch_shapes=[pltpu.VMEM((SOURCES * tok, d_model), BF16)] * 2
            + [pltpu.VMEM((rows_max + SUB, d_model), BF16)] * 3
            + [pltpu.VMEM((TILE, width), BF16)] * 3
            + [pltpu.VMEM((SOURCES * tok, d_model), F32),
               pltpu.SemaphoreType.DMA((n_u + n_dy,)),
               pltpu.SemaphoreType.DMA((5,))]),
        compiler_params=pltpu.CompilerParams(vmem_limit_bytes=VMEM_LIMIT),
        cost_estimate=cost(5, d_model, width, 3 * 2 * n_local * d_model * width),
        name='expert_input_grad',
    )(counts, *u_pieces, *dy_pieces, rank, gate, rank_t, gate_t, *weights)
    return out[:n_out], out[n_out:]


def expert_weight_grad(counts, kept, first, n_expert):
    _, _, d_model = kept[0].shape
    width = kept[2].shape[2]
    return pl.pallas_call(
        functools.partial(weight_grad_kernel, first),
        out_shape=jax.ShapeDtypeStruct((n_expert, 3, width, d_model), BF16),
        grid_spec=pltpu.PrefetchScalarGridSpec(
            num_scalar_prefetch=1,
            grid=(n_expert,),
            in_specs=[ANY] * 5,
            out_specs=per_expert((n_expert, 3, width, d_model)),
            scratch_shapes=[pltpu.VMEM((2, TILE, cols), BF16) for cols in (d_model, d_model, width, width, width)]
            + [pltpu.VMEM((3, width, d_model), F32), pltpu.SMEM((1,), jnp.int32), pltpu.SemaphoreType.DMA((2, 5))]),
        compiler_params=pltpu.CompilerParams(vmem_limit_bytes=VMEM_LIMIT),
        cost_estimate=cost(3 * n_expert // 4, d_model, width, 3 * 2 * n_expert * d_model * width),
        name='expert_weight_grad',
    )(counts, *kept)


def grad_sum(layer, n_layers, n_local, first, own, other, into):
    n_expert, _, width, d_model = own.shape
    rows = width // 2
    part = pl.BlockSpec((1, 3, rows, d_model), lambda e, r: (e, 0, r, 0))
    place = pl.BlockSpec((1, 1, rows, d_model), lambda e, r: (layer, first + e, r, 0))
    into = list(into or ())
    return pl.pallas_call(
        grad_sum_kernel,
        out_shape=[jax.ShapeDtypeStruct((n_layers, n_local, width, d_model), BF16)] * 3,
        grid=(n_expert, 2),
        in_specs=[part, part] + [ANY] * len(into),
        out_specs=[place] * 3,
        input_output_aliases={2 + i: i for i in range(len(into))},
        compiler_params=pltpu.CompilerParams(vmem_limit_bytes=VMEM_LIMIT),
        cost_estimate=pl.CostEstimate(flops=n_expert * 3 * width * d_model * 256, bytes_accessed=0, transcendentals=0),
        name='grad_sum',
    )(own, other, *into)


def hop(value, axis, step):
    n = lax.axis_size(axis)
    return lax.ppermute(value, axis, [(i, i ^ step) for i in range(n)])


def spread_direct(own):
    return [own, hop(own, 'ep', 1), hop(own, 'ep', 2), hop(own, 'ep', 3)]


def spread_relay(own):
    half = own.shape[0] // 2
    low, high = own[:half], own[half:]
    x_low, y_high = hop(low, 'ep', 1), hop(high, 'ep', 2)
    x_high, y_low = hop(high, 'ep', 1), hop(low, 'ep', 2)
    return [own, x_low, x_high, y_low, y_high, hop(x_low, 'ep', 2), hop(y_high, 'ep', 1)]


def to_f32(values):
    return [value.astype(F32) for value in values]


def collect_direct(base, parts):
    own, x_part, y_part, far = parts
    terms = to_f32([base, own, hop(x_part, 'ep', 1), hop(y_part, 'ep', 2), hop(far, 'ep', 3)])
    return sum(terms[1:], terms[0]).astype(BF16)


def collect_relay(base, parts):
    own, x_low, x_high, y_low, y_high, far_low, far_high = parts
    half = x_low.shape[0]
    via_x, via_y = hop(far_low, 'ep', 1), hop(far_high, 'ep', 2)
    got_x_low, got_y_high = hop(x_low, 'ep', 1), hop(y_high, 'ep', 2)
    got_y_low = hop((y_low.astype(F32) + via_x.astype(F32)).astype(BF16), 'ep', 2)
    got_x_high = hop((x_high.astype(F32) + via_y.astype(F32)).astype(BF16), 'ep', 1)
    low = to_f32([base[:half], own[:half], got_x_low, got_y_low])
    high = to_f32([base[half:], own[half:], got_x_high, got_y_high])
    return jnp.concatenate([sum(low[1:], low[0]), sum(high[1:], high[0])], axis=0).astype(BF16)


def take(value, index, rows):
    return lax.dynamic_slice_in_dim(value, index * rows, rows, 0)


def sum_everywhere(value):
    core, chip = lax.axis_index('dp'), lax.axis_index('ep')
    half = value.shape[0] // 2
    rows = half // 4
    other = hop(take(value, 1 - core, half), 'dp', 1)
    value = (take(value, core, half).astype(F32) + other.astype(F32)).astype(BF16)
    terms = [take(value, chip, rows)] + [hop(take(value, chip ^ step, rows), 'ep', step) for step in (1, 2, 3)]
    terms = to_f32(terms)
    own = sum(terms[1:], terms[0]).astype(BF16)
    near = spread_direct(own)
    value = jnp.stack(near)[chip ^ jnp.arange(4)].reshape(half, value.shape[1])
    other = hop(value, 'dp', 1)
    return jnp.where(core == 0, jnp.concatenate([value, other]), jnp.concatenate([other, value]))


def route_tables(expert_ids, gate_vals, n_local):
    packed = jnp.concatenate([expert_ids.astype(F32), gate_vals], axis=2)
    packed = jnp.stack(spread_direct(packed))
    top_k = expert_ids.shape[2]
    tok = expert_ids.shape[1]
    ids = packed[..., :top_k].astype(jnp.int32)
    gates = packed[..., top_k:]
    mine = lax.axis_index('ep') * n_local + jnp.arange(n_local)
    hits = ids[:, :, None] == mine[None, None, :, None, None]
    chosen = jnp.any(hits, axis=-1)
    gate = jnp.sum(jnp.where(hits, gates[:, :, None], 0.0), axis=-1)
    upto = (jnp.arange(tok)[:, None] <= jnp.arange(tok)[None, :]).astype(BF16)
    order = jnp.einsum('slet,tv->slev', chosen.astype(BF16), upto, preferred_element_type=F32)
    counts = order[..., -1].astype(jnp.int32)
    rank = jnp.where(chosen, order.astype(jnp.int32) - 1, -1)
    return [(counts[:, layer].T, rank[:, layer].transpose(1, 0, 2), gate[:, layer].transpose(1, 0, 2),
             rank[:, layer].transpose(1, 2, 0), gate[:, layer].transpose(1, 2, 0))
            for layer in range(expert_ids.shape[0])]


def after(value, *others):
    return lax.optimization_barrier((value, others))[0]


def mix_in(x_in, w_mix):
    return (x_in.astype(F32) + jnp.dot(x_in, w_mix, preferred_element_type=F32)).astype(BF16)


def mix_back(d_u, w_mix):
    return (d_u.astype(F32) + jnp.einsum('te,de->td', d_u, w_mix, preferred_element_type=F32)).astype(BF16)


def mix_grad(x_in, d_u):
    return jnp.einsum('td,te->de', x_in, d_u, preferred_element_type=F32).astype(BF16)


def solution(mesh):
    tok_spec = P(('dp', 'ep'), None)
    route_spec = P(None, ('dp', 'ep'), None)
    whole_spec = P(None, None, None)
    expert_spec = P(None, 'ep', None, None)

    def device_body(tokens, d_out, expert_ids, gate_vals, w_mix, w_gate, w_up, w_down):
        n_layers = w_mix.shape[0]
        n_local = w_gate.shape[1]
        last = n_layers - 1
        tok = tokens.shape[0]
        whole = [tok] * SOURCES
        halves = [tok] + [tok // 2] * (2 * SOURCES - 2)
        weights = (jnp.swapaxes(w_gate, 2, 3), jnp.swapaxes(w_up, 2, 3), w_down)

        x_in = [tokens]
        u_all = [spread_relay(mix_in(tokens, w_mix[0]))]
        tables = route_tables(expert_ids, gate_vals, n_local)
        for layer in range(last):
            parts = expert_forward(layer, u_all[layer], tables[layer], weights, halves)
            if layer == 0:
                dy_all = spread_direct(after(d_out, u_all[0]))
            x_in.append(collect_relay(u_all[layer][0], parts))
            u_all.append(spread_relay(mix_in(x_in[-1], w_mix[layer + 1])))

        d_y, grads, mixes, left = d_out, None, [None] * n_layers, []
        for layer in reversed(range(n_layers)):
            counts = tables[layer][0]
            parts, kept = expert_input_grad(layer, u_all[layer], dy_all, tables[layer], weights, whole)
            if layer == last:
                top = expert_forward(layer, after(u_all[layer], parts[0]), tables[layer], weights, whole)
                kept = after(kept, top)
            half = n_local // 2
            for first in (0, half):
                own = expert_weight_grad(counts, kept, first, half)
                left.append((layer, first, own, hop(own, 'dp', 1)))
            d_u = collect_direct(d_y, parts)
            mixes[layer] = sum_everywhere(mix_grad(x_in[layer], d_u))
            d_y = mix_back(d_u, w_mix[layer])
            if layer > 0:
                near = spread_direct(d_y)
                dy_all = after(near, left[-1][2])
            if layer == last:
                layer_out = collect_direct(u_all[last][0], after(top, near[1]))
        for layer, first, own, other in left:
            grads = grad_sum(layer, n_layers, n_local, first, own, other, grads)
        return (layer_out, d_y, jnp.stack(mixes), jnp.swapaxes(grads[0], 2, 3), jnp.swapaxes(grads[1], 2, 3), grads[2])

    return jax.shard_map(device_body, mesh=mesh,
                         in_specs=(tok_spec, tok_spec, route_spec, route_spec, whole_spec,
                                   expert_spec, expert_spec, expert_spec),
                         out_specs=(tok_spec, tok_spec, whole_spec, expert_spec, expert_spec, expert_spec),
                         check_vma=False)
```

time: 1740 us -> 722 us (0.41)
  matrix products: 475 us -> 9.55 us
  Pallas kernels: 0 us -> 344 us
  local copies, waits for them, and re-layouts: 359 us -> 20 us
  blocking collectives: 217 us -> 0 us
  waiting for transfers between devices: 451 us -> 248 us
  other arithmetic: 181 us -> 19.1 us
  starting transfers between devices: 35.7 us -> 75.1 us
    dot_general x24 -> x7, matrix products: 475 us -> 9.55 us  [the longest x2 3.93 us: mix_back(): jnp.einsum('te,de->td', d_u, w_mix, preferred_element_type=F32)]
    pallas_call x0 -> x12, Pallas kernels: none -> 344 us  [the longest x2 135 us: expert_input_grad(): pl.pallas_call(functools.partial(input_grad_kernel, n_u, n_dy, n_out, cap...]
    all_to_all x6 -> x0, waiting for transfers between devices: 284 us -> none  [the longest x2 96.9 us: layer_backward(): lax.all_to_all(d_recv, 'ep', 0, 0, tiled=True)]
    gather x16 -> x2, local copies, waits for them, and re-layouts: 254 us -> 1.17 us  [sum_everywhere(): value = jnp.stack(near)[chip ^ jnp.arange(4)].reshape(half, value.shape[1])]
    ppermute x0 -> x56, waiting for transfers between devices: none -> 248 us  [hop(): return lax.ppermute(value, axis, [(i, i ^ step) for i in range(n)])]
    all_to_all x2 -> x0, blocking collectives: 217 us -> none  [the longest x1 110 us: layer_forward(): recv_buf = lax.all_to_all(send_buf, 'ep', 0, 0, tiled=True)]
    psum x2 -> x0, waiting for transfers between devices: 167 us -> none  [the longest x1 141 us: layer_backward(): g_gate = lax.psum(g_gate, 'dp')]
    ppermute x0 -> x56, starting transfers between devices: none -> 75.1 us  [hop(): return lax.ppermute(value, axis, [(i, i ^ step) for i in range(n)])]
  transfers between devices with their start and end apart: 8 -> 56, of which waited for: 7 -> 35; matrix products, arithmetic and copies ran while one was open for 22% -> 6% of each run, Pallas kernels for 0% -> 26%
where the time goes in v1:
time: 722 us; the launch traced here: 718 us
  Pallas kernels  344 us (48%)
  waiting for transfers between devices  248 us (34%)
  starting transfers between devices  75.1 us (10%)
  local copies, waits for them, and re-layouts  20 us (3%)
  other arithmetic  19.1 us (3%)
  matrix products  9.55 us (1%)
    ppermute x56, waiting for transfers between devices, hop(): return lax.ppermute(value, axis, [(i, i ^ step) for i in range(n)])  248 us
    pallas_call x2, Pallas kernels, expert_input_grad(): pl.pallas_call(functools.partial(input_grad_kernel, n_u, n_dy, n_out, cap...  135 us
    pallas_call x2, Pallas kernels, expert_forward(): pl.pallas_call(functools.partial(forward_kernel, n_in, n_out, capacity),...  80.8 us
    pallas_call x4, Pallas kernels, expert_weight_grad(): pl.pallas_call(functools.partial(weight_grad_kernel, first), out_shape=ja...  77.3 us
    ppermute x56, starting transfers between devices, hop(): return lax.ppermute(value, axis, [(i, i ^ step) for i in range(n)])  75.1 us
    pallas_call x4, Pallas kernels, grad_sum(): pl.pallas_call(grad_sum_kernel, out_shape=[jax.ShapeDtypeStruct((n_layers...  51.3 us
  transfers between devices with their start and end apart: 56, of which 35 were waited for; matrix products, arithmetic and copies ran while one was open for 6% of the time, Pallas kernels for 26%

profile of v1, /device:TPU:0, one launch (start us, length us, event | category | flops | bytes accessed | tf_op | source)
XLA Modules:
  0.0 717.8 jit_solution(1478983939165260862)
XLA Ops:
  2.1 3.4 collective-permute-start.1
  6.9 2.5 add_convert_fusion.6.refs_1_
  11.1 2.0 collective-permute-start.6
  20.1 2.0 add_select_fusion
  25.4 8.5 %collective-permute-done.3.refs_2_ = bf16[256,768]{1,0:T(8,128)(2,1)} collective-permute-done((bf16[256,768]{1,0:T(8,128)(2,1)S(1)}, bf16[256,768]{1,0:T(8,128)(2,1)}, u32[]{:S(2)}, u32[]{:S(2)}) %collective-permute-start.3) | collective-permute-done | bytes 393248 | tf_op jit(solution)/shard_map/ppermute | solution.py:386
  41.9 40.6 %expert_forward.2 = (bf16[512,768]{1,0:T(8,128)(2,1)}, bf16[256,768]{1,0:T(8,128)(2,1)}, bf16[256,768]{1,0:T(8,128)(2,1)}, bf16[256,768]{1,0:T(8,128)(2,1)}, bf1...) custom-call(s32[4,4]{1,0:T(4,128)} %bitcast.113, bf16[512,768]{1,0:T(8,128)(2,1)} %copy-done.4, ...), custom_call_target="tpu_custom_call" | custom-call | flops 35672555520 | bytes 24772608 | tf_op jit(solution)/shard_map/expert_forward/pallas_call | solution.py:298
  82.7 2.0 collective-permute-start.12
  84.7 2.0 collective-permute-start.14
  86.7 8.1 %collective-permute-done.10 = bf16[256,768]{1,0:T(8,128)(2,1)S(1)} collective-permute-done((bf16[256,768]{1,0:T(8,128)(2,1)}, bf16[256,768]{1,0:T(8,128)(2,1)S(1)}, u32[]{:S(2)}, u32[]{:S(2)}) %collective-permute-start.10) | collective-permute-done | bytes 393248 | tf_op jit(solution)/shard_map/ppermute | solution.py:386
  97.1 2.0 collective-permute-start.13
  100.6 2.7 collective-permute-done.9
  105.0 2.5 collective-permute-start.21
  107.5 21.1 %collective-permute-done.11 = bf16[256,768]{1,0:T(8,128)(2,1)S(1)} collective-permute-done((bf16[256,768]{1,0:T(8,128)(2,1)S(1)}, bf16[256,768]{1,0:T(8,128)(2,1)S(1)}, u32[]{:S(2)}, u32[]{:S(2)}) %collective-permute-start.11) | collective-permute-done | bytes 393248 | tf_op jit(solution)/shard_map/ppermute | solution.py:386
  132.2 2.0 collective-permute-start.18
  134.2 2.0 collective-permute-start.16
  136.2 9.2 %collective-permute-done.22.refs_10_ = bf16[512,768]{1,0:T(8,128)(2,1)S(1)} collective-permute-done((bf16[512,768]{1,0:T(8,128)(2,1)}, bf16[512,768]{1,0:T(8,128)(2,1)S(1)}, u32[]{:S(2)}, u32[]{:S(2)}) %collective-permute-start.22) | collective-permute-done | bytes 786464 | tf_op jit(solution)/shard_map/ppermute | solution.py:386
  147.4 6.6 collective-permute-done.18.refs_5_
  154.0 2.0 collective-permute-start.20
  159.0 2.2 copy.71.refs_12_.refs_8_
  161.6 4.2 collective-permute-done.20.refs_7_
  165.8 67.6 %expert_input_grad.2 = (bf16[512,768]{1,0:T(8,128)(2,1)}, bf16[512,768]{1,0:T(8,128)(2,1)}, bf16[512,768]{1,0:T(8,128)(2,1)}, bf16[512,768]{1,0:T(8,128)(2,1)}, ...) custom-call(s32[4,4]{1,0:T(4,128)} %bitcast.117, ...), custom_call_target="tpu_custom_call" | custom-call | flops 59454259200 | bytes 24772608 | tf_op jit(solution)/shard_map/expert_input_grad/pallas_call | solution.py:324
  233.4 40.2 %expert_forward.3 = (bf16[512,768]{1,0:T(8,128)(2,1)}, bf16[512,768]{1,0:T(8,128)(2,1)}, bf16[512,768]{1,0:T(8,128)(2,1)}, bf16[512,768]{1,0:T(8,128)(2,1)}) custom-call(s32[4,4]{1,0:T(4,128)} %bitcast.118, bf16[512,768]{1,0:T(8,128)(2,1)} %copy-done.2, bf16[256,768]{1,0:T(8,128)(2,1)} %collective-permute-done.15.refs_2_, ...), custom_call_target="tpu_custom_call" | custom-call | flops 35672555520 | bytes 24772608 | tf_op jit(solution)/shard_map/expert_forward/pallas_call | solution.py:298
  277.1 24.2 %expert_weight_grad.7.own_ref = bf16[2,3,1344,768]{3,2,1,0:T(8,128)(2,1)} custom-call(s32[4,4]{1,0:T(4,128)} %bitcast.119, bf16[4,1536,768]{2,1,0:T(8,128)(2,1)} %get-tuple-element.100.x_hbm, bf16[4,1536,768]{2,1,0:T(8,128)(2,1)} %get-tuple-element.101.c_hbm, bf16[4,1536,1344]{2,1,0:T(8,128)(2,1)} %get-tuple-element.102.h_hbm, ...), custom_call_target="tpu_custom_call" | custom-call | flops 11890851840 | bytes 12386304 | tf_op jit(solution)/shard_map/expert_weight_grad/pallas_call | solution.py:349
  301.3 5.1 collective-permute-done.25
  306.5 2.3 add_convert_fusion.4
  313.2 13.8 %expert_weight_grad.4.own_ref = bf16[2,3,1344,768]{3,2,1,0:T(8,128)(2,1)} custom-call(s32[4,4]{1,0:T(4,128)} %bitcast.120, bf16[4,1536,768]{2,1,0:T(8,128)(2,1)} %get-tuple-element.100.x_hbm, bf16[4,1536,768]{2,1,0:T(8,128)(2,1)} %get-tuple-element.101.c_hbm, bf16[4,1536,1344]{2,1,0:T(8,128)(2,1)} %get-tuple-element.102.h_hbm, ...), custom_call_target="tpu_custom_call" | custom-call | flops 11890851840 | bytes 12386304 | tf_op jit(solution)/shard_map/expert_weight_grad/pallas_call | solution.py:349
  327.0 4.1 collective-permute-done.32.refs_11_
  331.1 14.1 %collective-permute-done.31.refs_10_ = bf16[512,768]{1,0:T(8,128)(2,1)} collective-permute-done((bf16[512,768]{1,0:T(8,128)(2,1)S(1)}, bf16[512,768]{1,0:T(8,128)(2,1)}, u32[]{:S(2)}, u32[]{:S(2)}) %collective-permute-start.31) | collective-permute-done | bytes 786464 | tf_op jit(solution)/shard_map/ppermute | solution.py:386
  345.2 67.3 %expert_input_grad.3 = (bf16[512,768]{1,0:T(8,128)(2,1)}, bf16[512,768]{1,0:T(8,128)(2,1)}, bf16[512,768]{1,0:T(8,128)(2,1)}, bf16[512,768]{1,0:T(8,128)(2,1)}, ...) custom-call(s32[4,4]{1,0:T(4,128)} %bitcast.114, ...), custom_call_target="tpu_custom_call" | custom-call | flops 59454259200 | bytes 24772608 | tf_op jit(solution)/shard_map/expert_input_grad/pallas_call | solution.py:324
  412.5 13.8 %expert_weight_grad.6.own_ref = bf16[2,3,1344,768]{3,2,1,0:T(8,128)(2,1)} custom-call(s32[4,4]{1,0:T(4,128)} %bitcast.115, bf16[4,1536,768]{2,1,0:T(8,128)(2,1)} %get-tuple-element.113.x_hbm, bf16[4,1536,768]{2,1,0:T(8,128)(2,1)} %get-tuple-element.114.c_hbm, bf16[4,1536,1344]{2,1,0:T(8,128)(2,1)} %get-tuple-element.115.h_hbm, ...), custom_call_target="tpu_custom_call" | custom-call | flops 11890851840 | bytes 12386304 | tf_op jit(solution)/shard_map/expert_weight_grad/pallas_call | solution.py:349
  426.4 25.5 %expert_weight_grad.5.own_ref = bf16[2,3,1344,768]{3,2,1,0:T(8,128)(2,1)} custom-call(s32[4,4]{1,0:T(4,128)} %bitcast.116, bf16[4,1536,768]{2,1,0:T(8,128)(2,1)} %get-tuple-element.113.x_hbm, bf16[4,1536,768]{2,1,0:T(8,128)(2,1)} %get-tuple-element.114.c_hbm, bf16[4,1536,1344]{2,1,0:T(8,128)(2,1)} %get-tuple-element.115.h_hbm, ...), custom_call_target="tpu_custom_call" | custom-call | flops 11890851840 | bytes 12386304 | tf_op jit(solution)/shard_map/expert_weight_grad/pallas_call | solution.py:349
  453.4 18.5 %collective-permute-done.44 = bf16[384,768]{1,0:T(8,128)(2,1)S(1)} collective-permute-done((bf16[384,768]{1,0:T(8,128)(2,1)S(1)}, bf16[384,768]{1,0:T(8,128)(2,1)S(1)}, u32[]{:S(2)}, u32[]{:S(2)}) %collective-permute-start.44) | collective-permute-done | bytes 589856 | tf_op jit(solution)/shard_map/ppermute | solution.py:386
  472.1 6.1 collective-permute-done.45
  478.2 3.8 collective-permute-start.47
  482.0 3.3 collective-permute-done.47
  487.0 3.4 collective-permute-done.46
  490.5 2.8 collective-permute-start.50
  493.3 3.4 collective-permute-done.50
  498.4 3.4 collective-permute-done.49
  503.1 5.4 collective-permute-done.48
  509.8 13.5 %collective-permute-done.33 = bf16[512,768]{1,0:T(8,128)(2,1)} collective-permute-done((bf16[512,768]{1,0:T(8,128)(2,1)}, bf16[512,768]{1,0:T(8,128)(2,1)}, u32[]{:S(2)}, u32[]{:S(2)}) %collective-permute-start.33) | collective-permute-done | bytes 786464 | tf_op jit(solution)/shard_map/ppermute | solution.py:386
  525.1 20.6 %collective-permute-done.34 = bf16[512,768]{1,0:T(8,128)(2,1)} collective-permute-done((bf16[512,768]{1,0:T(8,128)(2,1)}, bf16[512,768]{1,0:T(8,128)(2,1)}, u32[]{:S(2)}, u32[]{:S(2)}) %collective-permute-start.34) | collective-permute-done | bytes 786464 | tf_op jit(solution)/shard_map/ppermute | solution.py:386
  545.7 2.7 collective-permute-start.35
  549.1 9.8 %collective-permute-done.35 = bf16[512,768]{1,0:T(8,128)(2,1)} collective-permute-done((bf16[512,768]{1,0:T(8,128)(2,1)}, bf16[512,768]{1,0:T(8,128)(2,1)}, u32[]{:S(2)}, u32[]{:S(2)}) %collective-permute-start.35) | collective-permute-done | bytes 786464 | tf_op jit(solution)/shard_map/ppermute | solution.py:386
  558.9 2.2 add_convert_fusion.1
  566.0 18.0 %collective-permute-done.28 = bf16[512,768]{1,0:T(8,128)(2,1)S(1)} collective-permute-done((bf16[512,768]{1,0:T(8,128)(2,1)S(1)}, bf16[512,768]{1,0:T(8,128)(2,1)S(1)}, u32[]{:S(2)}, u32[]{:S(2)}) %collective-permute-start.28) | collective-permute-done | bytes 786464 | tf_op jit(solution)/shard_map/ppermute | solution.py:386
  585.6 3.7 collective-permute-done.37
  589.3 2.7 collective-permute-start.39
  592.0 3.3 collective-permute-done.39
  597.1 4.3 collective-permute-done.38
  603.3 14.0 %collective-permute-done.29 = bf16[512,768]{1,0:T(8,128)(2,1)S(1)} collective-permute-done((bf16[512,768]{1,0:T(8,128)(2,1)S(1)}, bf16[512,768]{1,0:T(8,128)(2,1)S(1)}, u32[]{:S(2)}, u32[]{:S(2)}) %collective-permute-start.29) | collective-permute-done | bytes 786464 | tf_op jit(solution)/shard_map/ppermute | solution.py:386
  618.2 4.3 collective-permute-start.42
  622.5 3.5 collective-permute-done.42
  626.0 2.4 collective-permute-start.41
  628.3 11.5 %collective-permute-done.41 = bf16[96,768]{1,0:T(8,128)(2,1)S(1)} collective-permute-done((bf16[96,768]{1,0:T(8,128)(2,1)S(1)}, bf16[96,768]{1,0:T(8,128)(2,1)S(1)}, u32[]{:S(2)}, u32[]{:S(2)}) %collective-permute-start.41) | collective-permute-done | bytes 147488 | tf_op jit(solution)/shard_map/ppermute | solution.py:386
  641.5 3.6 collective-permute-done.40
  645.0 3.0 collective-permute-start.30
  651.6 6.8 collective-permute-done.30
  658.4 3.1 add_convert_fusion
  661.6 2.6 add_convert_fusion.2
  666.2 12.8 %grad_sum.4 = (bf16[2,4,1344,768]{3,2,1,0:T(8,128)(2,1)}, bf16[2,4,1344,768]{3,2,1,0:T(8,128)(2,1)}, bf16[2,4,1344,768]{3,2,1,0:T(8,128)(2,1)}) custom-call(bf16[2,3,1344,768]{3,2,1,0:T(8,128)(2,1)} %expert_weight_grad.7.own_ref, bf16[2,3,1344,768]{3,2,1,0:T(8,128)(2,1)} %collective-permute-done.55.other_ref), custom_call_target="tpu_custom_call" | custom-call | flops 1585446912 | tf_op jit(solution)/shard_map/grad_sum/pallas_call | solution.py:371
  679.0 12.8 %grad_sum.5 = (bf16[2,4,1344,768]{3,2,1,0:T(8,128)(2,1)}, bf16[2,4,1344,768]{3,2,1,0:T(8,128)(2,1)}, bf16[2,4,1344,768]{3,2,1,0:T(8,128)(2,1)}) custom-call(bf16[2,3,1344,768]{3,2,1,0:T(8,128)(2,1)} %expert_weight_grad.4.own_ref, ...), custom_call_target="tpu_custom_call", output_to_operand_aliasing={{0}: (2, {}), {1}: (3, {}), {2}: (4, {})} | custom-call | flops 1585446912 | tf_op jit(solution)/shard_map/grad_sum/pallas_call | solution.py:371
  691.9 12.8 %grad_sum.6 = (bf16[2,4,1344,768]{3,2,1,0:T(8,128)(2,1)}, bf16[2,4,1344,768]{3,2,1,0:T(8,128)(2,1)}, bf16[2,4,1344,768]{3,2,1,0:T(8,128)(2,1)}) custom-call(bf16[2,3,1344,768]{3,2,1,0:T(8,128)(2,1)} %expert_weight_grad.6.own_ref, ...), custom_call_target="tpu_custom_call", output_to_operand_aliasing={{0}: (2, {}), {1}: (3, {}), {2}: (4, {})} | custom-call | flops 1585446912 | tf_op jit(solution)/shard_map/grad_sum/pallas_call | solution.py:371
  704.7 12.8 %grad_sum.7 = (bf16[2,4,1344,768]{3,2,1,0:T(8,128)(2,1)}, bf16[2,4,1344,768]{3,2,1,0:T(8,128)(2,1)}, bf16[2,4,1344,768]{3,2,1,0:T(8,128)(2,1)}) custom-call(bf16[2,3,1344,768]{3,2,1,0:T(8,128)(2,1)} %expert_weight_grad.5.own_ref, ...), custom_call_target="tpu_custom_call", output_to_operand_aliasing={{0}: (2, {}), {1}: (3, {}), {2}: (4, {})} | custom-call | flops 1585446912 | tf_op jit(solution)/shard_map/grad_sum/pallas_call | solution.py:371
  (185 shorter events, 73.7 us)
Async XLA Ops:
  2.1 12.5 %collective-permute-start.1 = (f32[2,512,8]{1,2,0:T(8,128)S(1)}, f32[2,512,8]{1,2,0:T(8,128)S(1)}, u32[]{:S(2)}, u32[]{:S(2)}) collective-permute-start(f32[2,512,8]{1,2,0:T(8,128)S(1)} %get-tuple-element.151), channel_id=1, source_target_pairs={{0,4},{2,6},{4,0},{6,2},{1,5},{3,7},{5,1},{7,3}} | collective-permute-start | bytes 98312 | tf_op jit(solution)/shard_map/ppermute | solution.py:386
  5.4 9.7 %collective-permute-start = (f32[2,512,8]{1,2,0:T(8,128)S(1)}, f32[2,512,8]{1,2,0:T(8,128)S(1)}, u32[]{:S(2)}, u32[]{:S(2)}) collective-permute-start(f32[2,512,8]{1,2,0:T(8,128)S(1)} %get-tuple-element.151), channel_id=1, source_target_pairs={{0,2},{2,0},{4,6},{6,4},{1,3},{3,1},{5,7},{7,5}} | collective-permute-start | bytes 98312 | tf_op jit(solution)/shard_map/ppermute | solution.py:386
  6.9 8.3 %collective-permute-start.2 = (f32[2,512,8]{1,2,0:T(8,128)S(1)}, f32[2,512,8]{1,2,0:T(8,128)S(1)}, u32[]{:S(2)}, u32[]{:S(2)}) collective-permute-start(f32[2,512,8]{1,2,0:T(8,128)S(1)} %get-tuple-element.151), channel_id=1, source_target_pairs={{0,6},{2,4},{4,2},{6,0},{1,7},{3,5},{5,3},{7,1}} | collective-permute-start | bytes 98312 | tf_op jit(solution)/shard_map/ppermute | solution.py:386
  11.1 12.3 %collective-permute-start.6 = (bf16[256,768]{1,0:T(8,128)(2,1)}, bf16[256,768]{1,0:T(8,128)(2,1)}, u32[]{:S(2)}, u32[]{:S(2)}) collective-permute-start(bf16[256,768]{1,0:T(8,128)(2,1)} %get-tuple-element.138), channel_id=1, source_target_pairs={{0,4},{2,6},{4,0},{6,2},{1,5},{3,7},{5,1},{7,3}} | collective-permute-start | bytes 1179656 | tf_op jit(solution)/shard_map/ppermute | solution.py:386
  13.1 25.6 %collective-permute-start.4 = (bf16[256,768]{1,0:T(8,128)(2,1)}, bf16[256,768]{1,0:T(8,128)(2,1)}, u32[]{:S(2)}, u32[]{:S(2)}) collective-permute-start(bf16[256,768]{1,0:T(8,128)(2,1)} %get-tuple-element.138), channel_id=1, source_target_pairs={{0,2},{2,0},{4,6},{6,4},{1,3},{3,1},{5,7},{7,5}} | collective-permute-start | bytes 1179656 | tf_op jit(solution)/shard_map/ppermute | solution.py:386
  14.6 19.2 %collective-permute-start.3 = (bf16[256,768]{1,0:T(8,128)(2,1)S(1)}, bf16[256,768]{1,0:T(8,128)(2,1)}, u32[]{:S(2)}, u32[]{:S(2)}) collective-permute-start(bf16[256,768]{1,0:T(8,128)(2,1)S(1)} %get-tuple-element.139), channel_id=1, source_target_pairs={{0,2},{2,0},{4,6},{6,4},{1,3},{3,1},{5,7},{7,5}} | collective-permute-start | bytes 1179656 | tf_op jit(solution)/shard_map/ppermute | solution.py:386
  15.2 23.5 %collective-permute-start.5 = (bf16[256,768]{1,0:T(8,128)(2,1)S(1)}, bf16[256,768]{1,0:T(8,128)(2,1)}, u32[]{:S(2)}, u32[]{:S(2)}) collective-permute-start(bf16[256,768]{1,0:T(8,128)(2,1)S(1)} %get-tuple-element.139), channel_id=1, source_target_pairs={{0,4},{2,6},{4,0},{6,2},{1,5},{3,7},{5,1},{7,3}} | collective-permute-start | bytes 1179656 | tf_op jit(solution)/shard_map/ppermute | solution.py:386
  23.4 16.6 %collective-permute-start.8 = (bf16[256,768]{1,0:T(8,128)(2,1)}, bf16[256,768]{1,0:T(8,128)(2,1)}, u32[]{:S(2)}, u32[]{:S(2)}) collective-permute-start(bf16[256,768]{1,0:T(8,128)(2,1)} %collective-permute-done.6.refs_5_), channel_id=1, source_target_pairs={{0,2},{2,0},{4,6},{6,4},{1,3},{3,1},{5,7},{7,5}} | collective-permute-start | bytes 1179656 | tf_op jit(solution)/shard_map/ppermute | solution.py:386
  33.9 8.1 %collective-permute-start.7 = (bf16[256,768]{1,0:T(8,128)(2,1)}, bf16[256,768]{1,0:T(8,128)(2,1)}, u32[]{:S(2)}, u32[]{:S(2)}) collective-permute-start(bf16[256,768]{1,0:T(8,128)(2,1)} %collective-permute-done.3.refs_2_), channel_id=1, source_target_pairs={{0,4},{2,6},{4,0},{6,2},{1,5},{3,7},{5,1},{7,3}} | collective-permute-start | bytes 1179656 | tf_op jit(solution)/shard_map/ppermute | solution.py:386
  82.6 46.0 %copy-start.5 = (bf16[512,768]{1,0:T(8,128)(2,1)S(1)}, bf16[512,768]{1,0:T(8,128)(2,1)}, u32[]{:S(2)}) copy-start(bf16[512,768]{1,0:T(8,128)(2,1)} %copy-done.4) | copy-start | bytes 2359300
  82.6 46.0 %copy-start.18 = (bf16[512,768]{1,0:T(8,128)(2,1)S(1)}, bf16[512,768]{1,0:T(8,128)(2,1)}, u32[]{:S(2)}) copy-start(bf16[512,768]{1,0:T(8,128)(2,1)} %get-tuple-element.68) | copy-start | bytes 2359300
  82.6 12.2 %collective-permute-start.10 = (bf16[256,768]{1,0:T(8,128)(2,1)}, bf16[256,768]{1,0:T(8,128)(2,1)S(1)}, u32[]{:S(2)}, u32[]{:S(2)}) collective-permute-start(bf16[256,768]{1,0:T(8,128)(2,1)} %get-tuple-element.71), channel_id=1, source_target_pairs={{0,2},{2,0},{4,6},{6,4},{1,3},{3,1},{5,7},{7,5}} | collective-permute-start | bytes 1179656 | tf_op jit(solution)/shard_map/ppermute | solution.py:386
  82.7 13.3 %collective-permute-start.12 = (bf16[256,768]{1,0:T(8,128)(2,1)}, bf16[256,768]{1,0:T(8,128)(2,1)S(1)}, u32[]{:S(2)}, u32[]{:S(2)}) collective-permute-start(bf16[256,768]{1,0:T(8,128)(2,1)} %get-tuple-element.73), channel_id=1, source_target_pairs={{0,4},{2,6},{4,0},{6,2},{1,5},{3,7},{5,1},{7,3}} | collective-permute-start | bytes 1179656 | tf_op jit(solution)/shard_map/ppermute | solution.py:386
  84.7 18.6 %collective-permute-start.9 = (bf16[256,768]{1,0:T(8,128)(2,1)}, bf16[256,768]{1,0:T(8,128)(2,1)S(1)}, u32[]{:S(2)}, u32[]{:S(2)}) collective-permute-start(bf16[256,768]{1,0:T(8,128)(2,1)} %get-tuple-element.69), channel_id=1, source_target_pairs={{0,2},{2,0},{4,6},{6,4},{1,3},{3,1},{5,7},{7,5}} | collective-permute-start | bytes 1179656 | tf_op jit(solution)/shard_map/ppermute | solution.py:386
  84.7 20.3 %collective-permute-start.14 = (bf16[256,768]{1,0:T(8,128)(2,1)}, bf16[256,768]{1,0:T(8,128)(2,1)S(1)}, u32[]{:S(2)}, u32[]{:S(2)}) collective-permute-start(bf16[256,768]{1,0:T(8,128)(2,1)} %get-tuple-element.74), channel_id=1, source_target_pairs={{0,4},{2,6},{4,0},{6,2},{1,5},{3,7},{5,1},{7,3}} | collective-permute-start | bytes 1179656 | tf_op jit(solution)/shard_map/ppermute | solution.py:386
  95.9 32.6 %collective-permute-start.11 = (bf16[256,768]{1,0:T(8,128)(2,1)S(1)}, bf16[256,768]{1,0:T(8,128)(2,1)S(1)}, u32[]{:S(2)}, u32[]{:S(2)}) collective-permute-start(bf16[256,768]{1,0:T(8,128)(2,1)S(1)} %add_convert_fusion.11), channel_id=1, source_target_pairs={{0,4},{2,6},{4,0},{6,2},{1,5},{3,7},{5,1},{7,3}} | collective-permute-start | bytes 1179656 | tf_op jit(solution)/shard_map/ppermute | solution.py:386
  97.1 31.5 %collective-permute-start.13 = (bf16[256,768]{1,0:T(8,128)(2,1)S(1)}, bf16[256,768]{1,0:T(8,128)(2,1)S(1)}, u32[]{:S(2)}, u32[]{:S(2)}) collective-permute-start(bf16[256,768]{1,0:T(8,128)(2,1)S(1)} %add_convert_fusion.9), channel_id=1, source_target_pairs={{0,2},{2,0},{4,6},{6,4},{1,3},{3,1},{5,7},{7,5}} | collective-permute-start | bytes 1179656 | tf_op jit(solution)/shard_map/ppermute | solution.py:386
  99.1 35.1 %collective-permute-start.23 = (bf16[512,768]{1,0:T(8,128)(2,1)}, bf16[512,768]{1,0:T(8,128)(2,1)S(1)}, u32[]{:S(2)}, u32[]{:S(2)}) collective-permute-start(bf16[512,768]{1,0:T(8,128)(2,1)} %refs_8_), channel_id=1, source_target_pairs={{0,6},{2,4},{4,2},{6,0},{1,7},{3,5},{5,3},{7,1}} | collective-permute-start | bytes 2359304 | tf_op jit(solution)/shard_map/ppermute | solution.py:386
  103.3 42.2 %collective-permute-start.22 = (bf16[512,768]{1,0:T(8,128)(2,1)}, bf16[512,768]{1,0:T(8,128)(2,1)S(1)}, u32[]{:S(2)}, u32[]{:S(2)}) collective-permute-start(bf16[512,768]{1,0:T(8,128)(2,1)} %refs_8_), channel_id=1, source_target_pairs={{0,4},{2,6},{4,0},{6,2},{1,5},{3,7},{5,1},{7,3}} | collective-permute-start | bytes 2359304 | tf_op jit(solution)/shard_map/ppermute | solution.py:386
  105.0 56.2 %collective-permute-start.21 = (bf16[512,768]{1,0:T(8,128)(2,1)}, bf16[512,768]{1,0:T(8,128)(2,1)}, u32[]{:S(2)}, u32[]{:S(2)}) collective-permute-start(bf16[512,768]{1,0:T(8,128)(2,1)} %refs_8_), channel_id=1, source_target_pairs={{0,2},{2,0},{4,6},{6,4},{1,3},{3,1},{5,7},{7,5}} | collective-permute-start | bytes 2359304 | tf_op jit(solution)/shard_map/ppermute | solution.py:386
  131.4 26.7 %copy-start.2 = (bf16[512,768]{1,0:T(8,128)(2,1)}, bf16[512,768]{1,0:T(8,128)(2,1)S(1)}, u32[]{:S(2)}) copy-start(bf16[512,768]{1,0:T(8,128)(2,1)S(1)} %add_convert_fusion.5.refs_1_) | copy-start | bytes 2359300
  132.2 21.8 %collective-permute-start.18 = (bf16[256,768]{1,0:T(8,128)(2,1)}, bf16[256,768]{1,0:T(8,128)(2,1)}, u32[]{:S(2)}, u32[]{:S(2)}) collective-permute-start(bf16[256,768]{1,0:T(8,128)(2,1)} %get-tuple-element.136), channel_id=1, source_target_pairs={{0,4},{2,6},{4,0},{6,2},{1,5},{3,7},{5,1},{7,3}} | collective-permute-start | bytes 1179656 | tf_op jit(solution)/shard_map/ppermute | solution.py:386
  134.2 21.8 %collective-permute-start.15 = (bf16[256,768]{1,0:T(8,128)(2,1)S(1)}, bf16[256,768]{1,0:T(8,128)(2,1)}, u32[]{:S(2)}, u32[]{:S(2)}) collective-permute-start(bf16[256,768]{1,0:T(8,128)(2,1)S(1)} %get-tuple-element.137), channel_id=1, source_target_pairs={{0,2},{2,0},{4,6},{6,4},{1,3},{3,1},{5,7},{7,5}} | collective-permute-start | bytes 1179656 | tf_op jit(solution)/shard_map/ppermute | solution.py:386
  134.2 27.4 %collective-permute-start.16 = (bf16[256,768]{1,0:T(8,128)(2,1)}, bf16[256,768]{1,0:T(8,128)(2,1)}, u32[]{:S(2)}, u32[]{:S(2)}) collective-permute-start(bf16[256,768]{1,0:T(8,128)(2,1)} %get-tuple-element.136), channel_id=1, source_target_pairs={{0,2},{2,0},{4,6},{6,4},{1,3},{3,1},{5,7},{7,5}} | collective-permute-start | bytes 1179656 | tf_op jit(solution)/shard_map/ppermute | solution.py:386
  145.4 16.1 %collective-permute-start.17 = (bf16[256,768]{1,0:T(8,128)(2,1)S(1)}, bf16[256,768]{1,0:T(8,128)(2,1)}, u32[]{:S(2)}, u32[]{:S(2)}) collective-permute-start(bf16[256,768]{1,0:T(8,128)(2,1)S(1)} %get-tuple-element.137), channel_id=1, source_target_pairs={{0,4},{2,6},{4,0},{6,2},{1,5},{3,7},{5,1},{7,3}} | collective-permute-start | bytes 1179656 | tf_op jit(solution)/shard_map/ppermute | solution.py:386
  154.0 11.8 %collective-permute-start.20 = (bf16[256,768]{1,0:T(8,128)(2,1)}, bf16[256,768]{1,0:T(8,128)(2,1)}, u32[]{:S(2)}, u32[]{:S(2)}) collective-permute-start(bf16[256,768]{1,0:T(8,128)(2,1)} %collective-permute-done.18.refs_5_), channel_id=1, source_target_pairs={{0,2},{2,0},{4,6},{6,4},{1,3},{3,1},{5,7},{7,5}} | collective-permute-start | bytes 1179656 | tf_op jit(solution)/shard_map/ppermute | solution.py:386
  156.0 9.8 %collective-permute-start.19 = (bf16[256,768]{1,0:T(8,128)(2,1)}, bf16[256,768]{1,0:T(8,128)(2,1)}, u32[]{:S(2)}, u32[]{:S(2)}) collective-permute-start(bf16[256,768]{1,0:T(8,128)(2,1)} %collective-permute-done.15.refs_2_), channel_id=1, source_target_pairs={{0,4},{2,6},{4,0},{6,2},{1,5},{3,7},{5,1},{7,3}} | collective-permute-start | bytes 1179656 | tf_op jit(solution)/shard_map/ppermute | solution.py:386
  273.6 27.7 %collective-permute-start.24 = (bf16[512,768]{1,0:T(8,128)(2,1)}, bf16[512,768]{1,0:T(8,128)(2,1)S(1)}, u32[]{:S(2)}, u32[]{:S(2)}) collective-permute-start(bf16[512,768]{1,0:T(8,128)(2,1)} %get-tuple-element.88), channel_id=1, source_target_pairs={{0,2},{2,0},{4,6},{6,4},{1,3},{3,1},{5,7},{7,5}} | collective-permute-start | bytes 2359304 | tf_op jit(solution)/shard_map/ppermute | solution.py:386
  275.3 31.1 %collective-permute-start.25 = (bf16[512,768]{1,0:T(8,128)(2,1)}, bf16[512,768]{1,0:T(8,128)(2,1)}, u32[]{:S(2)}, u32[]{:S(2)}) collective-permute-start(bf16[512,768]{1,0:T(8,128)(2,1)} %get-tuple-element.89), channel_id=1, source_target_pairs={{0,4},{2,6},{4,0},{6,2},{1,5},{3,7},{5,1},{7,3}} | collective-permute-start | bytes 2359304 | tf_op jit(solution)/shard_map/ppermute | solution.py:386
  275.3 31.1 %copy-start.16 = (bf16[512,768]{1,0:T(8,128)(2,1)S(1)}, bf16[512,768]{1,0:T(8,128)(2,1)}, u32[]{:S(2)}) copy-start(bf16[512,768]{1,0:T(8,128)(2,1)} %get-tuple-element.76) | copy-start | bytes 2359300
  275.4 31.1 %collective-permute-start.26 = (bf16[512,768]{1,0:T(8,128)(2,1)}, bf16[512,768]{1,0:T(8,128)(2,1)}, u32[]{:S(2)}, u32[]{:S(2)}) collective-permute-start(bf16[512,768]{1,0:T(8,128)(2,1)} %get-tuple-element.90), channel_id=1, source_target_pairs={{0,6},{2,4},{4,2},{6,0},{1,7},{3,5},{5,3},{7,1}} | collective-permute-start | bytes 2359304 | tf_op jit(solution)/shard_map/ppermute | solution.py:386
  301.3 364.9 %collective-permute-start.55 = (bf16[2,3,1344,768]{3,2,1,0:T(8,128)(2,1)}, bf16[2,3,1344,768]{3,2,1,0:T(8,128)(2,1)}, u32[]{:S(2)}, u32[]{:S(2)}) collective-permute-start(bf16[2,3,1344,768]{3,2,1,0:T(8,128)(2,1)} %expert_weight_grad.7.own_ref), channel_id=1, source_target_pairs={{0,1},{1,0},{2,3},{3,2},{4,5},{5,4},{6,7},{7,6}} | collective-permute-start | bytes 37158920 | tf_op jit(solution)/shard_map/ppermute | solution.py:386
  309.7 21.4 %collective-permute-start.32 = (bf16[512,768]{1,0:T(8,128)(2,1)S(1)}, bf16[512,768]{1,0:T(8,128)(2,1)}, u32[]{:S(2)}, u32[]{:S(2)}) collective-permute-start(bf16[512,768]{1,0:T(8,128)(2,1)S(1)} %add_convert_fusion.3.refs_8_), channel_id=1, source_target_pairs={{0,6},{2,4},{4,2},{6,0},{1,7},{3,5},{5,3},{7,1}} | collective-permute-start | bytes 2359304 | tf_op jit(solution)/shard_map/ppermute | solution.py:386
  310.9 34.4 %collective-permute-start.31 = (bf16[512,768]{1,0:T(8,128)(2,1)S(1)}, bf16[512,768]{1,0:T(8,128)(2,1)}, u32[]{:S(2)}, u32[]{:S(2)}) collective-permute-start(bf16[512,768]{1,0:T(8,128)(2,1)S(1)} %add_convert_fusion.3.refs_8_), channel_id=1, source_target_pairs={{0,4},{2,6},{4,0},{6,2},{1,5},{3,7},{5,1},{7,3}} | collective-permute-start | bytes 2359304 | tf_op jit(solution)/shard_map/ppermute | solution.py:386
  311.7 33.5 %collective-permute-start.27 = (bf16[512,768]{1,0:T(8,128)(2,1)S(1)}, bf16[512,768]{1,0:T(8,128)(2,1)}, u32[]{:S(2)}, u32[]{:S(2)}) collective-permute-start(bf16[512,768]{1,0:T(8,128)(2,1)S(1)} %add_convert_fusion.3.refs_8_), channel_id=1, source_target_pairs={{0,2},{2,0},{4,6},{6,4},{1,3},{3,1},{5,7},{7,5}} | collective-permute-start | bytes 2359304 | tf_op jit(solution)/shard_map/ppermute | solution.py:386
  327.0 352.0 %collective-permute-start.54 = (bf16[2,3,1344,768]{3,2,1,0:T(8,128)(2,1)}, bf16[2,3,1344,768]{3,2,1,0:T(8,128)(2,1)}, u32[]{:S(2)}, u32[]{:S(2)}) collective-permute-start(bf16[2,3,1344,768]{3,2,1,0:T(8,128)(2,1)} %expert_weight_grad.4.own_ref), channel_id=1, source_target_pairs={{0,1},{1,0},{2,3},{3,2},{4,5},{5,4},{6,7},{7,6}} | collective-permute-start | bytes 37158920 | tf_op jit(solution)/shard_map/ppermute | solution.py:386
  426.4 265.5 %collective-permute-start.53 = (bf16[2,3,1344,768]{3,2,1,0:T(8,128)(2,1)}, bf16[2,3,1344,768]{3,2,1,0:T(8,128)(2,1)}, u32[]{:S(2)}, u32[]{:S(2)}) collective-permute-start(bf16[2,3,1344,768]{3,2,1,0:T(8,128)(2,1)} %expert_weight_grad.6.own_ref), channel_id=1, source_target_pairs={{0,1},{1,0},{2,3},{3,2},{4,5},{5,4},{6,7},{7,6}} | collective-permute-start | bytes 37158920 | tf_op jit(solution)/shard_map/ppermute | solution.py:386
  451.9 252.8 %collective-permute-start.52 = (bf16[2,3,1344,768]{3,2,1,0:T(8,128)(2,1)}, bf16[2,3,1344,768]{3,2,1,0:T(8,128)(2,1)}, u32[]{:S(2)}, u32[]{:S(2)}) collective-permute-start(bf16[2,3,1344,768]{3,2,1,0:T(8,128)(2,1)} %expert_weight_grad.5.own_ref), channel_id=1, source_target_pairs={{0,1},{1,0},{2,3},{3,2},{4,5},{5,4},{6,7},{7,6}} | collective-permute-start | bytes 37158920 | tf_op jit(solution)/shard_map/ppermute | solution.py:386
  453.2 18.7 %collective-permute-start.44 = (bf16[384,768]{1,0:T(8,128)(2,1)S(1)}, bf16[384,768]{1,0:T(8,128)(2,1)S(1)}, u32[]{:S(2)}, u32[]{:S(2)}) collective-permute-start(bf16[384,768]{1,0:T(8,128)(2,1)S(1)} %constant_dynamic-slice_fusion.3), channel_id=1, source_target_pairs={{0,1},{1,0},{2,3},{3,2},{4,5},{5,4},{6,7},{7,6}} | collective-permute-start | bytes 1769480 | tf_op jit(solution)/shard_map/ppermute | solution.py:386
  472.1 86.8 %copy-start.8 = (bf16[512,768]{1,0:T(8,128)(2,1)S(1)}, bf16[512,768]{1,0:T(8,128)(2,1)}, u32[]{:S(2)}) copy-start(bf16[512,768]{1,0:T(8,128)(2,1)} %copy-done.7) | copy-start | bytes 2359300
  472.1 86.8 %copy-start.9 = (bf16[512,768]{1,0:T(8,128)(2,1)S(1)}, bf16[512,768]{1,0:T(8,128)(2,1)}, u32[]{:S(2)}) copy-start(bf16[512,768]{1,0:T(8,128)(2,1)} %get-tuple-element.109) | copy-start | bytes 2359300
  472.1 6.1 collective-permute-start.45
  478.2 7.0 collective-permute-start.47
  485.3 5.1 collective-permute-start.46
  490.5 6.2 collective-permute-start.50
  496.7 5.1 collective-permute-start.49
  501.8 6.7 collective-permute-start.48
  508.5 14.8 %collective-permute-start.33 = (bf16[512,768]{1,0:T(8,128)(2,1)}, bf16[512,768]{1,0:T(8,128)(2,1)}, u32[]{:S(2)}, u32[]{:S(2)}) collective-permute-start(bf16[512,768]{1,0:T(8,128)(2,1)} %get-tuple-element.110), channel_id=1, source_target_pairs={{0,2},{2,0},{4,6},{6,4},{1,3},{3,1},{5,7},{7,5}} | collective-permute-start | bytes 2359304 | tf_op jit(solution)/shard_map/ppermute | solution.py:386
  523.3 22.3 %collective-permute-start.34 = (bf16[512,768]{1,0:T(8,128)(2,1)}, bf16[512,768]{1,0:T(8,128)(2,1)}, u32[]{:S(2)}, u32[]{:S(2)}) collective-permute-start(bf16[512,768]{1,0:T(8,128)(2,1)} %get-tuple-element.111), channel_id=1, source_target_pairs={{0,4},{2,6},{4,0},{6,2},{1,5},{3,7},{5,1},{7,3}} | collective-permute-start | bytes 2359304 | tf_op jit(solution)/shard_map/ppermute | solution.py:386
  545.7 13.2 %collective-permute-start.35 = (bf16[512,768]{1,0:T(8,128)(2,1)}, bf16[512,768]{1,0:T(8,128)(2,1)}, u32[]{:S(2)}, u32[]{:S(2)}) collective-permute-start(bf16[512,768]{1,0:T(8,128)(2,1)} %get-tuple-element.112), channel_id=1, source_target_pairs={{0,6},{2,4},{4,2},{6,0},{1,7},{3,5},{5,3},{7,1}} | collective-permute-start | bytes 2359304 | tf_op jit(solution)/shard_map/ppermute | solution.py:386
  558.9 3.1 collective-permute-start.51
  562.0 39.4 %copy-start.30 = (bf16[512,768]{1,0:T(8,128)(2,1)S(1)}, bf16[512,768]{1,0:T(8,128)(2,1)}, u32[]{:S(2)}) copy-start(bf16[512,768]{1,0:T(8,128)(2,1)} %get-tuple-element.93) | copy-start | bytes 2359300
  562.0 41.3 %copy-start.19 = (bf16[384,768]{1,0:T(8,128)(2,1)}, bf16[384,768]{1,0:T(8,128)(2,1)S(1)}, u32[]{:S(2)}) copy-start(bf16[384,768]{1,0:T(8,128)(2,1)S(1)} %collective-permute-done.51) | copy-start | bytes 1769476
  562.0 2.1 collective-permute-start.36
  564.2 19.8 %collective-permute-start.28 = (bf16[512,768]{1,0:T(8,128)(2,1)S(1)}, bf16[512,768]{1,0:T(8,128)(2,1)S(1)}, u32[]{:S(2)}, u32[]{:S(2)}) collective-permute-start(bf16[512,768]{1,0:T(8,128)(2,1)S(1)} %copy-done.31), channel_id=1, source_target_pairs={{0,2},{2,0},{4,6},{6,4},{1,3},{3,1},{5,7},{7,5}} | collective-permute-start | bytes 2359304 | tf_op jit(solution)/shard_map/ppermute | solution.py:386
  584.0 5.3 collective-permute-start.37
  589.3 6.0 collective-permute-start.39
  595.3 6.1 collective-permute-start.38
  601.4 15.9 %collective-permute-start.29 = (bf16[512,768]{1,0:T(8,128)(2,1)S(1)}, bf16[512,768]{1,0:T(8,128)(2,1)S(1)}, u32[]{:S(2)}, u32[]{:S(2)}) collective-permute-start(bf16[512,768]{1,0:T(8,128)(2,1)S(1)} %copy-done.30), channel_id=1, source_target_pairs={{0,4},{2,6},{4,0},{6,2},{1,5},{3,7},{5,1},{7,3}} | collective-permute-start | bytes 2359304 | tf_op jit(solution)/shard_map/ppermute | solution.py:386
  618.2 7.8 %collective-permute-start.42 = (bf16[96,768]{1,0:T(8,128)(2,1)S(1)}, bf16[96,768]{1,0:T(8,128)(2,1)S(1)}, u32[]{:S(2)}, u32[]{:S(2)}) collective-permute-start(bf16[96,768]{1,0:T(8,128)(2,1)S(1)} %add_convert_fusion.13), channel_id=1, source_target_pairs={{0,6},{2,4},{4,2},{6,0},{1,7},{3,5},{5,3},{7,1}} | collective-permute-start | bytes 442376 | tf_op jit(solution)/shard_map/ppermute | solution.py:386
  626.0 13.9 %collective-permute-start.41 = (bf16[96,768]{1,0:T(8,128)(2,1)S(1)}, bf16[96,768]{1,0:T(8,128)(2,1)S(1)}, u32[]{:S(2)}, u32[]{:S(2)}) collective-permute-start(bf16[96,768]{1,0:T(8,128)(2,1)S(1)} %add_convert_fusion.13), channel_id=1, source_target_pairs={{0,4},{2,6},{4,0},{6,2},{1,5},{3,7},{5,1},{7,3}} | collective-permute-start | bytes 442376 | tf_op jit(solution)/shard_map/ppermute | solution.py:386
  639.9 5.1 collective-permute-start.40
  645.0 13.3 %collective-permute-start.30 = (bf16[512,768]{1,0:T(8,128)(2,1)}, bf16[512,768]{1,0:T(8,128)(2,1)}, u32[]{:S(2)}, u32[]{:S(2)}) collective-permute-start(bf16[512,768]{1,0:T(8,128)(2,1)} %get-tuple-element.94), channel_id=1, source_target_pairs={{0,6},{2,4},{4,2},{6,0},{1,7},{3,5},{5,3},{7,1}} | collective-permute-start | bytes 2359304 | tf_op jit(solution)/shard_map/ppermute | solution.py:386
  658.4 5.8 collective-permute-start.43
  (26 other events, 240.3 us)

commit v2 on v1

--- a/solution.py
+++ b/solution.py
@@ -150,24 +150,42 @@
         put_out(acc, outs)
 
 
-def input_grad_kernel(n_u, n_dy, n_out, capacity, *refs):
+def input_grad_kernel(n_u, n_dy, n_out, capacity, forward, *refs):
     count_ref, refs = refs[0], refs[1:]
     u_pieces, refs = refs[:n_u], refs[n_u:]
     dy_pieces, refs = refs[:n_dy], refs[n_dy:]
     rank_ref, gate_ref, rank_t_ref, gate_t_ref, wg_ref, wu_ref, wd_ref = refs[:7]
-    outs, refs = refs[7:7 + n_out], refs[7 + n_out:]
+    refs = refs[7:]
+    outs, refs = refs[:n_out], refs[n_out:]
+    tops, refs = (refs[:n_out], refs[n_out:]) if forward else ((), refs)
     kept, refs = refs[:5], refs[5:]
-    u_buf, dy_buf, x_buf, c_buf, v_buf, h_buf, da_buf, db_buf, acc, sems, keep_sems = refs
+    u_buf, dy_buf, x_buf, c_buf, v_buf, h_buf, da_buf, db_buf, acc, slot_ref, sems, keep_sems = refs[:12]
     expert = pl.program_id(0)
+    last = expert == pl.num_programs(0) - 1
     tok = rank_t_ref.shape[1]
+    if forward:
+        o_buf, top_acc = refs[12:]
+
+    def keep_cols(tile, slot):
+        return [pltpu.make_async_copy(src.at[slot], dst.at[expert, tile_span(tile)], keep_sems.at[slot, i])
+                for i, (src, dst) in enumerate(((h_buf, kept[2]), (da_buf, kept[3]), (db_buf, kept[4])))]
+
+    def keep_rows(tile):
+        span = tile_span(tile)
+        return [pltpu.make_async_copy(src.at[span], dst.at[expert, span], keep_sems.at[2, i])
+                for i, (src, dst) in enumerate(((x_buf, kept[0]), (c_buf, kept[1])))]
 
     @pl.when(expert == 0)
     def _():
         copies = fetch(u_pieces, u_buf, sems, 0) + fetch(dy_pieces, dy_buf, sems, n_u)
         for copy in copies:
             copy.start()
+        slot_ref[0] = 0
         acc[...] = jnp.zeros_like(acc)
         v_buf[...] = jnp.zeros_like(v_buf)
+        if forward:
+            top_acc[...] = jnp.zeros_like(top_acc)
+            o_buf[...] = jnp.zeros_like(o_buf)
         for copy in copies:
             copy.wait()
 
@@ -184,36 +202,51 @@
 
     gather(counts, offsets, rank_ref, capacity, tok, write)
 
-    def tile_step(tile, carry):
+    def tile_step(tile, slot):
         span = tile_span(tile)
-        keep = [pltpu.make_async_copy(src, dst.at[expert, span], keep_sems.at[i]) for i, (src, dst) in enumerate(
-            zip((x_buf.at[span], c_buf.at[span], h_buf, da_buf, db_buf), kept))]
-        keep[0].start()
-        keep[1].start()
+        rows_out = keep_rows(tile)
+        for copy in rows_out:
+            copy.start()
         rows = x_buf[span, :]
         grads = c_buf[span, :]
-        for cols in f_chunks(h_buf.shape[1]):
+        for cols in f_chunks(h_buf.shape[2]):
             pre_gate = dot_nt(rows, wg_ref[0, 0, cols, :])
             pre_up = dot_nt(rows, wu_ref[0, 0, cols, :])
             d_hid = dot_nt(grads, wd_ref[0, 0, cols, :])
             act, slope = silu_parts(pre_gate)
-            h_buf[:, cols] = (act * pre_up).astype(BF16)
-            da_buf[:, cols] = (d_hid * pre_up * slope).astype(BF16)
-            db_buf[:, cols] = (d_hid * act).astype(BF16)
-        for copy in keep[2:]:
+            h_buf[slot, :, cols] = (act * pre_up).astype(BF16)
+            da_buf[slot, :, cols] = (d_hid * pre_up * slope).astype(BF16)
+            db_buf[slot, :, cols] = (d_hid * act).astype(BF16)
+        cols_out = keep_cols(tile, slot)
+        for copy in cols_out:
             copy.start()
-        v_buf[span, :] = (dot_nn(da_buf[...], wg_ref[0, 0]) + dot_nn(db_buf[...], wu_ref[0, 0])).astype(BF16)
-        for copy in keep:
+        if forward:
+            o_buf[span, :] = dot_nn(h_buf[slot], wd_ref[0, 0]).astype(BF16)
+        v_buf[span, :] = (dot_nn(da_buf[slot], wg_ref[0, 0]) + dot_nn(db_buf[slot], wu_ref[0, 0])).astype(BF16)
+        for copy in rows_out:
             copy.wait()
-        return carry
-
-    lax.fori_loop(0, tiles, tile_step, 0)
+
+        @pl.when(tile > 0)
+        def _():
+            for copy in keep_cols(tile - 1, 1 - slot):
+                copy.wait()
+
+        return 1 - slot
+
+    slot = lax.fori_loop(0, tiles, tile_step, slot_ref[0])
+    slot_ref[0] = slot
 
     combine(counts, offsets, rank_t_ref, gate_t_ref, v_buf, acc, capacity, tok)
-
-    @pl.when(expert == pl.num_programs(0) - 1)
+    if forward:
+        combine(counts, offsets, rank_t_ref, gate_t_ref, o_buf, top_acc, capacity, tok)
+    for copy in keep_cols(tiles - 1, 1 - slot):
+        copy.wait()
+
+    @pl.when(last)
     def _():
         put_out(acc, outs)
+        if forward:
+            put_out(top_acc, tops)
 
 
 def weight_grad_kernel(first, count_ref, x_hbm, c_hbm, h_hbm, da_hbm, db_hbm, out_ref,
@@ -316,31 +349,34 @@
     )(counts, *u_pieces, rank, rank_t, gate_t, *weights)
 
 
-def expert_input_grad(layer, u_pieces, dy_pieces, tables, weights, out_rows):
+def expert_input_grad(layer, u_pieces, dy_pieces, tables, weights, out_rows, forward):
     tok, capacity, rows_max, n_local, width, d_model = sizes(tables, weights)
     counts, rank, gate, rank_t, gate_t = tables
     n_u, n_dy, n_out = len(u_pieces), len(dy_pieces), len(out_rows)
     kept = [jax.ShapeDtypeStruct((n_local, rows_max, cols), BF16) for cols in (d_model, d_model, width, width, width)]
+    sums = [jax.ShapeDtypeStruct((rows, d_model), BF16) for rows in out_rows] * (1 + forward)
+    row_buf = pltpu.VMEM((rows_max + SUB, d_model), BF16)
+    token_acc = pltpu.VMEM((SOURCES * tok, d_model), F32)
     out = pl.pallas_call(
-        functools.partial(input_grad_kernel, n_u, n_dy, n_out, capacity),
-        out_shape=[jax.ShapeDtypeStruct((rows, d_model), BF16) for rows in out_rows] + kept,
+        functools.partial(input_grad_kernel, n_u, n_dy, n_out, capacity, forward),
+        out_shape=sums + kept,
         grid_spec=pltpu.PrefetchScalarGridSpec(
             num_scalar_prefetch=1,
             grid=(n_local,),
             in_specs=[ANY] * (n_u + n_dy) + [per_expert(t.shape) for t in (rank, gate, rank_t, gate_t)]
             + [layer_weight(layer, w.shape) for w in weights],
-            out_specs=[VMEM] * n_out + [ANY] * 5,
-            scratch_shapes=[pltpu.VMEM((SOURCES * tok, d_model), BF16)] * 2
-            + [pltpu.VMEM((rows_max + SUB, d_model), BF16)] * 3
-            + [pltpu.VMEM((TILE, width), BF16)] * 3
-            + [pltpu.VMEM((SOURCES * tok, d_model), F32),
+            out_specs=[VMEM] * len(sums) + [ANY] * 5,
+            scratch_shapes=[pltpu.VMEM((SOURCES * tok, d_model), BF16)] * 2 + [row_buf] * 3
+            + [pltpu.VMEM((2, TILE, width), BF16)] * 3
+            + [token_acc, pltpu.SMEM((1,), jnp.int32),
                pltpu.SemaphoreType.DMA((n_u + n_dy,)),
-               pltpu.SemaphoreType.DMA((5,))]),
+               pltpu.SemaphoreType.DMA((3, 3))]
+            + [row_buf, token_acc] * forward),
         compiler_params=pltpu.CompilerParams(vmem_limit_bytes=VMEM_LIMIT),
-        cost_estimate=cost(5, d_model, width, 3 * 2 * n_local * d_model * width),
+        cost_estimate=cost(5 + forward, d_model, width, 3 * 2 * n_local * d_model * width),
         name='expert_input_grad',
     )(counts, *u_pieces, *dy_pieces, rank, gate, rank_t, gate_t, *weights)
-    return out[:n_out], out[n_out:]
+    return out[:n_out], out[n_out:len(sums)], out[len(sums):]
 
 
 def expert_weight_grad(counts, kept, first, n_expert):
@@ -500,27 +536,27 @@
             x_in.append(collect_relay(u_all[layer][0], parts))
             u_all.append(spread_relay(mix_in(x_in[-1], w_mix[layer + 1])))
 
-        d_y, grads, mixes, left = d_out, None, [None] * n_layers, []
+        d_y, grads, mixes = d_out, None, [None] * n_layers
         for layer in reversed(range(n_layers)):
             counts = tables[layer][0]
-            parts, kept = expert_input_grad(layer, u_all[layer], dy_all, tables[layer], weights, whole)
-            if layer == last:
-                top = expert_forward(layer, after(u_all[layer], parts[0]), tables[layer], weights, whole)
-                kept = after(kept, top)
+            parts, top, kept = expert_input_grad(layer, u_all[layer], dy_all, tables[layer], weights, whole,
+                                                 layer == last)
             half = n_local // 2
+            left = []
             for first in (0, half):
                 own = expert_weight_grad(counts, kept, first, half)
-                left.append((layer, first, own, hop(own, 'dp', 1)))
+                left.append((first, own, hop(own, 'dp', 1)))
             d_u = collect_direct(d_y, parts)
             mixes[layer] = sum_everywhere(mix_grad(x_in[layer], d_u))
             d_y = mix_back(d_u, w_mix[layer])
             if layer > 0:
-                near = spread_direct(d_y)
-                dy_all = after(near, left[-1][2])
+                dy_all = spread_direct(d_y)
+            for first, own, other in left:
+                grads = grad_sum(layer, n_layers, n_local, first, own, other, grads)
+            if layer > 0:
+                dy_all = after(dy_all, grads)
             if layer == last:
-                layer_out = collect_direct(u_all[last][0], after(top, near[1]))
-        for layer, first, own, other in left:
-            grads = grad_sum(layer, n_layers, n_local, first, own, other, grads)
+                layer_out = collect_direct(u_all[last][0], after(top, dy_all[1]))
         return (layer_out, d_y, jnp.stack(mixes), jnp.swapaxes(grads[0], 2, 3), jnp.swapaxes(grads[1], 2, 3), grads[2])
 
     return jax.shard_map(device_body, mesh=mesh,

time: 722 us -> 618 us (0.86)
  waiting for transfers between devices: 248 us -> 200 us
  Pallas kernels: 344 us -> 304 us
  starting transfers between devices: 75.1 us -> 58.4 us
    ppermute x56, waiting for transfers between devices: 248 us -> 200 us  [hop(): return lax.ppermute(value, axis, [(i, i ^ step) for i in range(n)])]
    pallas_call x2 -> x1, Pallas kernels: 80.8 us -> 40.3 us  [expert_forward(): pl.pallas_call(functools.partial(forward_kernel, n_in, n_out, capacity),...]
    ppermute x56, starting transfers between devices: 75.1 us -> 58.4 us  [hop(): return lax.ppermute(value, axis, [(i, i ^ step) for i in range(n)])]
  transfers between devices with their start and end apart: 56 -> 56, of which waited for: 35 -> 29; matrix products, arithmetic and copies ran while one was open for 6% -> 7% of each run, Pallas kernels for 26% -> 13%
where the time goes in v2:
time: 618 us; the launch traced here: 614 us
  Pallas kernels  304 us (49%)
  waiting for transfers between devices  200 us (32%)
  starting transfers between devices  58.4 us (9%)
  local copies, waits for them, and re-layouts  21.3 us (3%)
  other arithmetic  20.3 us (3%)
  matrix products  9.5 us (2%)
    ppermute x56, waiting for transfers between devices, hop(): return lax.ppermute(value, axis, [(i, i ^ step) for i in range(n)])  200 us
    pallas_call x2, Pallas kernels, expert_input_grad(): pl.pallas_call(functools.partial(input_grad_kernel, n_u, n_dy, n_out, cap...  135 us
    pallas_call x4, Pallas kernels, expert_weight_grad(): pl.pallas_call(functools.partial(weight_grad_kernel, first), out_shape=ja...  77.3 us
    ppermute x56, starting transfers between devices, hop(): return lax.ppermute(value, axis, [(i, i ^ step) for i in range(n)])  58.4 us
    pallas_call x4, Pallas kernels, grad_sum(): pl.pallas_call(grad_sum_kernel, out_shape=[jax.ShapeDtypeStruct((n_layers...  51.3 us
    pallas_call x1, Pallas kernels, expert_forward(): pl.pallas_call(functools.partial(forward_kernel, n_in, n_out, capacity),...  40.3 us
  transfers between devices with their start and end apart: 56, of which 29 were waited for; matrix products, arithmetic and copies ran while one was open for 7% of the time, Pallas kernels for 13%

profile of v2, /device:TPU:0, one launch (start us, length us, event | category | flops | bytes accessed | tf_op | source)
XLA Modules:
  0.0 614.1 jit_solution(9026981385608345923)
XLA Ops:
  2.1 3.4 collective-permute-start.1
  6.9 2.5 add_convert_fusion.6.refs_1_
  11.1 2.0 collective-permute-start.6
  18.0 2.0 copy.62
  20.1 2.0 add_select_fusion
  23.4 2.0 collective-permute-start.8
  25.4 8.5 %collective-permute-done.3.refs_2_ = bf16[256,768]{1,0:T(8,128)(2,1)} collective-permute-done((bf16[256,768]{1,0:T(8,128)(2,1)S(1)}, bf16[256,768]{1,0:T(8,128)(2,1)}, u32[]{:S(2)}, u32[]{:S(2)}) %collective-permute-start.3) | collective-permute-done | bytes 393248 | tf_op jit(solution)/shard_map/ppermute | solution.py:422
  35.9 1.8 slice_bitcast_fusion.1
  40.0 1.9 collective-permute-done.7.refs_6_
  41.9 40.3 %expert_forward.1 = (bf16[512,768]{1,0:T(8,128)(2,1)}, bf16[256,768]{1,0:T(8,128)(2,1)}, bf16[256,768]{1,0:T(8,128)(2,1)}, bf16[256,768]{1,0:T(8,128)(2,1)}, bf1...) custom-call(s32[4,4]{1,0:T(4,128)} %bitcast.112, bf16[512,768]{1,0:T(8,128)(2,1)} %copy-done.5, ...), custom_call_target="tpu_custom_call" | custom-call | flops 35672555520 | bytes 24772608 | tf_op jit(solution)/shard_map/expert_forward/pallas_call | solution.py:331
  82.3 2.0 collective-permute-start.12
  84.3 2.0 collective-permute-start.14
  86.3 8.1 %collective-permute-done.10 = bf16[256,768]{1,0:T(8,128)(2,1)S(1)} collective-permute-done((bf16[256,768]{1,0:T(8,128)(2,1)}, bf16[256,768]{1,0:T(8,128)(2,1)S(1)}, u32[]{:S(2)}, u32[]{:S(2)}) %collective-permute-start.10) | collective-permute-done | bytes 393248 | tf_op jit(solution)/shard_map/ppermute | solution.py:422
  96.7 2.0 collective-permute-start.13
  100.2 2.7 collective-permute-done.9
  102.9 1.7 collective-permute-done.14
  104.6 2.5 collective-permute-start.21
  107.1 21.1 %collective-permute-done.11 = bf16[256,768]{1,0:T(8,128)(2,1)S(1)} collective-permute-done((bf16[256,768]{1,0:T(8,128)(2,1)S(1)}, bf16[256,768]{1,0:T(8,128)(2,1)S(1)}, u32[]{:S(2)}, u32[]{:S(2)}) %collective-permute-start.11) | collective-permute-done | bytes 393248 | tf_op jit(solution)/shard_map/ppermute | solution.py:422
  131.8 2.0 collective-permute-start.18
  133.8 2.0 collective-permute-start.16
  135.8 9.3 %collective-permute-done.22.refs_10_ = bf16[512,768]{1,0:T(8,128)(2,1)S(1)} collective-permute-done((bf16[512,768]{1,0:T(8,128)(2,1)}, bf16[512,768]{1,0:T(8,128)(2,1)S(1)}, u32[]{:S(2)}, u32[]{:S(2)}) %collective-permute-start.22) | collective-permute-done | bytes 786464 | tf_op jit(solution)/shard_map/ppermute | solution.py:422
  145.1 2.0 collective-permute-start.17
  147.0 6.6 %collective-permute-done.18.refs_5_ = bf16[256,768]{1,0:T(8,128)(2,1)} collective-permute-done((bf16[256,768]{1,0:T(8,128)(2,1)}, bf16[256,768]{1,0:T(8,128)(2,1)}, u32[]{:S(2)}, u32[]{:S(2)}) %collective-permute-start.18) | collective-permute-done | bytes 393248 | tf_op jit(solution)/shard_map/ppermute | solution.py:422
  153.6 2.0 collective-permute-start.20
  158.5 2.7 collective-permute-done.16.refs_3_
  161.2 4.2 collective-permute-done.20.refs_7_
  165.5 71.3 %expert_input_grad.2 = (bf16[512,768]{1,0:T(8,128)(2,1)}, bf16[512,768]{1,0:T(8,128)(2,1)}, bf16[512,768]{1,0:T(8,128)(2,1)}, bf16[512,768]{1,0:T(8,128)(2,1)}, ...) custom-call(s32[4,4]{1,0:T(4,128)} %bitcast.116, ...), custom_call_target="tpu_custom_call" | custom-call | flops 71345111040 | bytes 24772608 | tf_op jit(solution)/shard_map/expert_input_grad/pallas_call | solution.py:360
  236.7 24.1 %expert_weight_grad.5.own_ref = bf16[2,3,1344,768]{3,2,1,0:T(8,128)(2,1)} custom-call(s32[4,4]{1,0:T(4,128)} %bitcast.117, bf16[4,1536,768]{2,1,0:T(8,128)(2,1)} %get-tuple-element.72.x_hbm, bf16[4,1536,768]{2,1,0:T(8,128)(2,1)} %get-tuple-element.73.c_hbm, bf16[4,1536,1344]{2,1,0:T(8,128)(2,1)} %get-tuple-element.74.h_hbm, ...), custom_call_target="tpu_custom_call" | custom-call | flops 11890851840 | bytes 12386304 | tf_op jit(solution)/shard_map/expert_weight_grad/pallas_call | solution.py:385
  260.9 14.0 %expert_weight_grad.4.own_ref = bf16[2,3,1344,768]{3,2,1,0:T(8,128)(2,1)} custom-call(s32[4,4]{1,0:T(4,128)} %bitcast.118, bf16[4,1536,768]{2,1,0:T(8,128)(2,1)} %get-tuple-element.72.x_hbm, bf16[4,1536,768]{2,1,0:T(8,128)(2,1)} %get-tuple-element.73.c_hbm, bf16[4,1536,1344]{2,1,0:T(8,128)(2,1)} %get-tuple-element.74.h_hbm, ...), custom_call_target="tpu_custom_call" | custom-call | flops 11890851840 | bytes 12386304 | tf_op jit(solution)/shard_map/expert_weight_grad/pallas_call | solution.py:385
  275.3 1.7 collective-permute-start.24
  277.0 1.8 collective-permute-start.26
  278.7 17.1 %collective-permute-done.24 = bf16[512,768]{1,0:T(8,128)(2,1)S(1)} collective-permute-done((bf16[512,768]{1,0:T(8,128)(2,1)}, bf16[512,768]{1,0:T(8,128)(2,1)S(1)}, u32[]{:S(2)}, u32[]{:S(2)}) %collective-permute-start.24) | collective-permute-done | bytes 786464 | tf_op jit(solution)/shard_map/ppermute | solution.py:422
  295.9 17.5 %collective-permute-done.25 = bf16[512,768]{1,0:T(8,128)(2,1)S(1)} collective-permute-done((bf16[512,768]{1,0:T(8,128)(2,1)}, bf16[512,768]{1,0:T(8,128)(2,1)S(1)}, u32[]{:S(2)}, u32[]{:S(2)}) %collective-permute-start.25) | collective-permute-done | bytes 786464 | tf_op jit(solution)/shard_map/ppermute | solution.py:422
  313.4 1.8 add_convert_fusion.4
  318.0 1.7 collective-permute-start.27
  320.6 12.8 %grad_sum.4 = (bf16[2,4,1344,768]{3,2,1,0:T(8,128)(2,1)}, bf16[2,4,1344,768]{3,2,1,0:T(8,128)(2,1)}, bf16[2,4,1344,768]{3,2,1,0:T(8,128)(2,1)}) custom-call(bf16[2,3,1344,768]{3,2,1,0:T(8,128)(2,1)} %expert_weight_grad.5.own_ref, bf16[2,3,1344,768]{3,2,1,0:T(8,128)(2,1)} %collective-permute-done.31.other_ref), custom_call_target="tpu_custom_call" | custom-call | flops 1585446912 | tf_op jit(solution)/shard_map/grad_sum/pallas_call | solution.py:407
  333.5 12.8 %grad_sum.5 = (bf16[2,4,1344,768]{3,2,1,0:T(8,128)(2,1)}, bf16[2,4,1344,768]{3,2,1,0:T(8,128)(2,1)}, bf16[2,4,1344,768]{3,2,1,0:T(8,128)(2,1)}) custom-call(bf16[2,3,1344,768]{3,2,1,0:T(8,128)(2,1)} %expert_weight_grad.4.own_ref, ...), custom_call_target="tpu_custom_call", output_to_operand_aliasing={{0}: (2, {}), {1}: (3, {}), {2}: (4, {})} | custom-call | flops 1585446912 | tf_op jit(solution)/shard_map/grad_sum/pallas_call | solution.py:407
  346.3 6.5 %collective-permute-done.28.refs_10_ = bf16[512,768]{1,0:T(8,128)(2,1)} collective-permute-done((bf16[512,768]{1,0:T(8,128)(2,1)S(1)}, bf16[512,768]{1,0:T(8,128)(2,1)}, u32[]{:S(2)}, u32[]{:S(2)}) %collective-permute-start.28) | collective-permute-done | bytes 786464 | tf_op jit(solution)/shard_map/ppermute | solution.py:422
  352.8 63.7 %expert_input_grad.3 = (bf16[512,768]{1,0:T(8,128)(2,1)}, bf16[512,768]{1,0:T(8,128)(2,1)}, bf16[512,768]{1,0:T(8,128)(2,1)}, bf16[512,768]{1,0:T(8,128)(2,1)}, ...) custom-call(s32[4,4]{1,0:T(4,128)} %bitcast.113, ...), custom_call_target="tpu_custom_call" | custom-call | flops 59454259200 | bytes 24772608 | tf_op jit(solution)/shard_map/expert_input_grad/pallas_call | solution.py:360
  416.5 13.7 %expert_weight_grad.7.own_ref = bf16[2,3,1344,768]{3,2,1,0:T(8,128)(2,1)} custom-call(s32[4,4]{1,0:T(4,128)} %bitcast.114, bf16[4,1536,768]{2,1,0:T(8,128)(2,1)} %get-tuple-element.95.x_hbm, bf16[4,1536,768]{2,1,0:T(8,128)(2,1)} %get-tuple-element.96.c_hbm, bf16[4,1536,1344]{2,1,0:T(8,128)(2,1)} %get-tuple-element.97.h_hbm, ...), custom_call_target="tpu_custom_call" | custom-call | flops 11890851840 | bytes 12386304 | tf_op jit(solution)/shard_map/expert_weight_grad/pallas_call | solution.py:385
  430.3 25.4 %expert_weight_grad.6.own_ref = bf16[2,3,1344,768]{3,2,1,0:T(8,128)(2,1)} custom-call(s32[4,4]{1,0:T(4,128)} %bitcast.115, bf16[4,1536,768]{2,1,0:T(8,128)(2,1)} %get-tuple-element.95.x_hbm, bf16[4,1536,768]{2,1,0:T(8,128)(2,1)} %get-tuple-element.96.c_hbm, bf16[4,1536,1344]{2,1,0:T(8,128)(2,1)} %get-tuple-element.97.h_hbm, ...), custom_call_target="tpu_custom_call" | custom-call | flops 11890851840 | bytes 12386304 | tf_op jit(solution)/shard_map/expert_weight_grad/pallas_call | solution.py:385
  458.0 17.7 %collective-permute-done.46 = bf16[384,768]{1,0:T(8,128)(2,1)S(1)} collective-permute-done((bf16[384,768]{1,0:T(8,128)(2,1)S(1)}, bf16[384,768]{1,0:T(8,128)(2,1)S(1)}, u32[]{:S(2)}, u32[]{:S(2)}) %collective-permute-start.46) | collective-permute-done | bytes 589856 | tf_op jit(solution)/shard_map/ppermute | solution.py:422
  476.6 3.8 collective-permute-start.37
  482.3 16.7 %collective-permute-done.37 = bf16[512,768]{1,0:T(8,128)(2,1)} collective-permute-done((bf16[512,768]{1,0:T(8,128)(2,1)}, bf16[512,768]{1,0:T(8,128)(2,1)}, u32[]{:S(2)}, u32[]{:S(2)}) %collective-permute-start.37) | collective-permute-done | bytes 786464 | tf_op jit(solution)/shard_map/ppermute | solution.py:422
  499.1 2.6 add_convert_fusion.1
  502.6 2.9 collective-permute-start.49
  505.6 4.8 collective-permute-done.49
  510.4 3.2 collective-permute-done.48
  514.5 1.8 collective-permute-start.52
  516.3 1.7 collective-permute-start.50
  520.0 2.2 collective-permute-done.52
  522.2 2.2 collective-permute-done.51
  528.2 4.3 collective-permute-done.41
  532.6 3.0 collective-permute-done.40
  537.0 1.7 collective-permute-start.32
  539.2 4.1 collective-permute-done.44
  543.3 1.7 collective-permute-start.42
  547.1 15.4 %collective-permute-done.42 = bf16[96,768]{1,0:T(8,128)(2,1)S(1)} collective-permute-done((bf16[96,768]{1,0:T(8,128)(2,1)S(1)}, bf16[96,768]{1,0:T(8,128)(2,1)S(1)}, u32[]{:S(2)}, u32[]{:S(2)}) %collective-permute-start.42) | collective-permute-done | bytes 147488 | tf_op jit(solution)/shard_map/ppermute | solution.py:422
  566.4 3.1 add_convert_fusion
  569.5 11.9 %collective-permute-done.33 = bf16[512,768]{1,0:T(8,128)(2,1)} collective-permute-done((bf16[512,768]{1,0:T(8,128)(2,1)}, bf16[512,768]{1,0:T(8,128)(2,1)}, u32[]{:S(2)}, u32[]{:S(2)}) %collective-permute-start.33) | collective-permute-done | bytes 786464 | tf_op jit(solution)/shard_map/ppermute | solution.py:422
  581.4 1.8 collective-permute-done.34
  583.2 3.0 add_convert_fusion.2
  588.3 12.8 %grad_sum.6 = (bf16[2,4,1344,768]{3,2,1,0:T(8,128)(2,1)}, bf16[2,4,1344,768]{3,2,1,0:T(8,128)(2,1)}, bf16[2,4,1344,768]{3,2,1,0:T(8,128)(2,1)}) custom-call(bf16[2,3,1344,768]{3,2,1,0:T(8,128)(2,1)} %expert_weight_grad.7.own_ref, ...), custom_call_target="tpu_custom_call", output_to_operand_aliasing={{0}: (2, {}), {1}: (3, {}), {2}: (4, {})} | custom-call | flops 1585446912 | tf_op jit(solution)/shard_map/grad_sum/pallas_call | solution.py:407
  601.1 12.8 %grad_sum.7 = (bf16[2,4,1344,768]{3,2,1,0:T(8,128)(2,1)}, bf16[2,4,1344,768]{3,2,1,0:T(8,128)(2,1)}, bf16[2,4,1344,768]{3,2,1,0:T(8,128)(2,1)}) custom-call(bf16[2,3,1344,768]{3,2,1,0:T(8,128)(2,1)} %expert_weight_grad.6.own_ref, ...), custom_call_target="tpu_custom_call", output_to_operand_aliasing={{0}: (2, {}), {1}: (3, {}), {2}: (4, {})} | custom-call | flops 1585446912 | tf_op jit(solution)/shard_map/grad_sum/pallas_call | solution.py:407
  (178 shorter events, 52.3 us)
Async XLA Ops:
  2.1 12.5 %collective-permute-start.1 = (f32[2,512,8]{1,2,0:T(8,128)S(1)}, f32[2,512,8]{1,2,0:T(8,128)S(1)}, u32[]{:S(2)}, u32[]{:S(2)}) collective-permute-start(f32[2,512,8]{1,2,0:T(8,128)S(1)} %get-tuple-element.127), channel_id=1, source_target_pairs={{0,4},{2,6},{4,0},{6,2},{1,5},{3,7},{5,1},{7,3}} | collective-permute-start | bytes 98312 | tf_op jit(solution)/shard_map/ppermute | solution.py:422
  5.4 9.7 %collective-permute-start = (f32[2,512,8]{1,2,0:T(8,128)S(1)}, f32[2,512,8]{1,2,0:T(8,128)S(1)}, u32[]{:S(2)}, u32[]{:S(2)}) collective-permute-start(f32[2,512,8]{1,2,0:T(8,128)S(1)} %get-tuple-element.127), channel_id=1, source_target_pairs={{0,2},{2,0},{4,6},{6,4},{1,3},{3,1},{5,7},{7,5}} | collective-permute-start | bytes 98312 | tf_op jit(solution)/shard_map/ppermute | solution.py:422
  6.9 8.3 %collective-permute-start.2 = (f32[2,512,8]{1,2,0:T(8,128)S(1)}, f32[2,512,8]{1,2,0:T(8,128)S(1)}, u32[]{:S(2)}, u32[]{:S(2)}) collective-permute-start(f32[2,512,8]{1,2,0:T(8,128)S(1)} %get-tuple-element.127), channel_id=1, source_target_pairs={{0,6},{2,4},{4,2},{6,0},{1,7},{3,5},{5,3},{7,1}} | collective-permute-start | bytes 98312 | tf_op jit(solution)/shard_map/ppermute | solution.py:422
  11.1 12.3 %collective-permute-start.6 = (bf16[256,768]{1,0:T(8,128)(2,1)}, bf16[256,768]{1,0:T(8,128)(2,1)}, u32[]{:S(2)}, u32[]{:S(2)}) collective-permute-start(bf16[256,768]{1,0:T(8,128)(2,1)} %get-tuple-element.114), channel_id=1, source_target_pairs={{0,4},{2,6},{4,0},{6,2},{1,5},{3,7},{5,1},{7,3}} | collective-permute-start | bytes 1179656 | tf_op jit(solution)/shard_map/ppermute | solution.py:422
  13.1 25.6 %collective-permute-start.4 = (bf16[256,768]{1,0:T(8,128)(2,1)}, bf16[256,768]{1,0:T(8,128)(2,1)}, u32[]{:S(2)}, u32[]{:S(2)}) collective-permute-start(bf16[256,768]{1,0:T(8,128)(2,1)} %get-tuple-element.114), channel_id=1, source_target_pairs={{0,2},{2,0},{4,6},{6,4},{1,3},{3,1},{5,7},{7,5}} | collective-permute-start | bytes 1179656 | tf_op jit(solution)/shard_map/ppermute | solution.py:422
  14.6 19.2 %collective-permute-start.3 = (bf16[256,768]{1,0:T(8,128)(2,1)S(1)}, bf16[256,768]{1,0:T(8,128)(2,1)}, u32[]{:S(2)}, u32[]{:S(2)}) collective-permute-start(bf16[256,768]{1,0:T(8,128)(2,1)S(1)} %get-tuple-element.115), channel_id=1, source_target_pairs={{0,2},{2,0},{4,6},{6,4},{1,3},{3,1},{5,7},{7,5}} | collective-permute-start | bytes 1179656 | tf_op jit(solution)/shard_map/ppermute | solution.py:422
  15.2 23.5 %collective-permute-start.5 = (bf16[256,768]{1,0:T(8,128)(2,1)S(1)}, bf16[256,768]{1,0:T(8,128)(2,1)}, u32[]{:S(2)}, u32[]{:S(2)}) collective-permute-start(bf16[256,768]{1,0:T(8,128)(2,1)S(1)} %get-tuple-element.115), channel_id=1, source_target_pairs={{0,4},{2,6},{4,0},{6,2},{1,5},{3,7},{5,1},{7,3}} | collective-permute-start | bytes 1179656 | tf_op jit(solution)/shard_map/ppermute | solution.py:422
  23.4 16.6 %collective-permute-start.8 = (bf16[256,768]{1,0:T(8,128)(2,1)}, bf16[256,768]{1,0:T(8,128)(2,1)}, u32[]{:S(2)}, u32[]{:S(2)}) collective-permute-start(bf16[256,768]{1,0:T(8,128)(2,1)} %collective-permute-done.6.refs_5_), channel_id=1, source_target_pairs={{0,2},{2,0},{4,6},{6,4},{1,3},{3,1},{5,7},{7,5}} | collective-permute-start | bytes 1179656 | tf_op jit(solution)/shard_map/ppermute | solution.py:422
  33.9 8.1 %collective-permute-start.7 = (bf16[256,768]{1,0:T(8,128)(2,1)}, bf16[256,768]{1,0:T(8,128)(2,1)}, u32[]{:S(2)}, u32[]{:S(2)}) collective-permute-start(bf16[256,768]{1,0:T(8,128)(2,1)} %collective-permute-done.3.refs_2_), channel_id=1, source_target_pairs={{0,4},{2,6},{4,0},{6,2},{1,5},{3,7},{5,1},{7,3}} | collective-permute-start | bytes 1179656 | tf_op jit(solution)/shard_map/ppermute | solution.py:422
  82.2 46.0 %copy-start.6 = (bf16[512,768]{1,0:T(8,128)(2,1)S(1)}, bf16[512,768]{1,0:T(8,128)(2,1)}, u32[]{:S(2)}) copy-start(bf16[512,768]{1,0:T(8,128)(2,1)} %copy-done.5) | copy-start | bytes 2359300
  82.2 46.0 %copy-start.14 = (bf16[512,768]{1,0:T(8,128)(2,1)S(1)}, bf16[512,768]{1,0:T(8,128)(2,1)}, u32[]{:S(2)}) copy-start(bf16[512,768]{1,0:T(8,128)(2,1)} %get-tuple-element.56) | copy-start | bytes 2359300
  82.3 12.2 %collective-permute-start.10 = (bf16[256,768]{1,0:T(8,128)(2,1)}, bf16[256,768]{1,0:T(8,128)(2,1)S(1)}, u32[]{:S(2)}, u32[]{:S(2)}) collective-permute-start(bf16[256,768]{1,0:T(8,128)(2,1)} %get-tuple-element.59), channel_id=1, source_target_pairs={{0,2},{2,0},{4,6},{6,4},{1,3},{3,1},{5,7},{7,5}} | collective-permute-start | bytes 1179656 | tf_op jit(solution)/shard_map/ppermute | solution.py:422
  82.3 13.3 %collective-permute-start.12 = (bf16[256,768]{1,0:T(8,128)(2,1)}, bf16[256,768]{1,0:T(8,128)(2,1)S(1)}, u32[]{:S(2)}, u32[]{:S(2)}) collective-permute-start(bf16[256,768]{1,0:T(8,128)(2,1)} %get-tuple-element.61), channel_id=1, source_target_pairs={{0,4},{2,6},{4,0},{6,2},{1,5},{3,7},{5,1},{7,3}} | collective-permute-start | bytes 1179656 | tf_op jit(solution)/shard_map/ppermute | solution.py:422
  84.3 18.6 %collective-permute-start.9 = (bf16[256,768]{1,0:T(8,128)(2,1)}, bf16[256,768]{1,0:T(8,128)(2,1)S(1)}, u32[]{:S(2)}, u32[]{:S(2)}) collective-permute-start(bf16[256,768]{1,0:T(8,128)(2,1)} %get-tuple-element.57), channel_id=1, source_target_pairs={{0,2},{2,0},{4,6},{6,4},{1,3},{3,1},{5,7},{7,5}} | collective-permute-start | bytes 1179656 | tf_op jit(solution)/shard_map/ppermute | solution.py:422
  84.3 20.3 %collective-permute-start.14 = (bf16[256,768]{1,0:T(8,128)(2,1)}, bf16[256,768]{1,0:T(8,128)(2,1)S(1)}, u32[]{:S(2)}, u32[]{:S(2)}) collective-permute-start(bf16[256,768]{1,0:T(8,128)(2,1)} %get-tuple-element.62), channel_id=1, source_target_pairs={{0,4},{2,6},{4,0},{6,2},{1,5},{3,7},{5,1},{7,3}} | collective-permute-start | bytes 1179656 | tf_op jit(solution)/shard_map/ppermute | solution.py:422
  95.6 32.6 %collective-permute-start.11 = (bf16[256,768]{1,0:T(8,128)(2,1)S(1)}, bf16[256,768]{1,0:T(8,128)(2,1)S(1)}, u32[]{:S(2)}, u32[]{:S(2)}) collective-permute-start(bf16[256,768]{1,0:T(8,128)(2,1)S(1)} %add_convert_fusion.11), channel_id=1, source_target_pairs={{0,4},{2,6},{4,0},{6,2},{1,5},{3,7},{5,1},{7,3}} | collective-permute-start | bytes 1179656 | tf_op jit(solution)/shard_map/ppermute | solution.py:422
  96.7 31.5 %collective-permute-start.13 = (bf16[256,768]{1,0:T(8,128)(2,1)S(1)}, bf16[256,768]{1,0:T(8,128)(2,1)S(1)}, u32[]{:S(2)}, u32[]{:S(2)}) collective-permute-start(bf16[256,768]{1,0:T(8,128)(2,1)S(1)} %add_convert_fusion.9), channel_id=1, source_target_pairs={{0,2},{2,0},{4,6},{6,4},{1,3},{3,1},{5,7},{7,5}} | collective-permute-start | bytes 1179656 | tf_op jit(solution)/shard_map/ppermute | solution.py:422
  98.7 35.1 %collective-permute-start.23 = (bf16[512,768]{1,0:T(8,128)(2,1)}, bf16[512,768]{1,0:T(8,128)(2,1)S(1)}, u32[]{:S(2)}, u32[]{:S(2)}) collective-permute-start(bf16[512,768]{1,0:T(8,128)(2,1)} %refs_8_), channel_id=1, source_target_pairs={{0,6},{2,4},{4,2},{6,0},{1,7},{3,5},{5,3},{7,1}} | collective-permute-start | bytes 2359304 | tf_op jit(solution)/shard_map/ppermute | solution.py:422
  102.9 42.2 %collective-permute-start.22 = (bf16[512,768]{1,0:T(8,128)(2,1)}, bf16[512,768]{1,0:T(8,128)(2,1)S(1)}, u32[]{:S(2)}, u32[]{:S(2)}) collective-permute-start(bf16[512,768]{1,0:T(8,128)(2,1)} %refs_8_), channel_id=1, source_target_pairs={{0,4},{2,6},{4,0},{6,2},{1,5},{3,7},{5,1},{7,3}} | collective-permute-start | bytes 2359304 | tf_op jit(solution)/shard_map/ppermute | solution.py:422
  104.6 53.9 %collective-permute-start.21 = (bf16[512,768]{1,0:T(8,128)(2,1)}, bf16[512,768]{1,0:T(8,128)(2,1)}, u32[]{:S(2)}, u32[]{:S(2)}) collective-permute-start(bf16[512,768]{1,0:T(8,128)(2,1)} %refs_8_), channel_id=1, source_target_pairs={{0,2},{2,0},{4,6},{6,4},{1,3},{3,1},{5,7},{7,5}} | collective-permute-start | bytes 2359304 | tf_op jit(solution)/shard_map/ppermute | solution.py:422
  131.0 26.6 %copy-start.3 = (bf16[512,768]{1,0:T(8,128)(2,1)}, bf16[512,768]{1,0:T(8,128)(2,1)S(1)}, u32[]{:S(2)}) copy-start(bf16[512,768]{1,0:T(8,128)(2,1)S(1)} %add_convert_fusion.5.refs_1_) | copy-start | bytes 2359300
  131.0 26.6 %copy-start.2 = (s32[4,4,512]{1,2,0:T(8,128)S(1)}, s32[4,4,512]{1,2,0:T(8,128)}, u32[]{:S(2)}) copy-start(s32[4,4,512]{1,2,0:T(8,128)} %get-tuple-element.108) | copy-start | bytes 98308
  131.8 21.8 %collective-permute-start.18 = (bf16[256,768]{1,0:T(8,128)(2,1)}, bf16[256,768]{1,0:T(8,128)(2,1)}, u32[]{:S(2)}, u32[]{:S(2)}) collective-permute-start(bf16[256,768]{1,0:T(8,128)(2,1)} %get-tuple-element.112), channel_id=1, source_target_pairs={{0,4},{2,6},{4,0},{6,2},{1,5},{3,7},{5,1},{7,3}} | collective-permute-start | bytes 1179656 | tf_op jit(solution)/shard_map/ppermute | solution.py:422
  133.8 21.8 %collective-permute-start.15 = (bf16[256,768]{1,0:T(8,128)(2,1)S(1)}, bf16[256,768]{1,0:T(8,128)(2,1)}, u32[]{:S(2)}, u32[]{:S(2)}) collective-permute-start(bf16[256,768]{1,0:T(8,128)(2,1)S(1)} %get-tuple-element.113), channel_id=1, source_target_pairs={{0,2},{2,0},{4,6},{6,4},{1,3},{3,1},{5,7},{7,5}} | collective-permute-start | bytes 1179656 | tf_op jit(solution)/shard_map/ppermute | solution.py:422
  133.8 27.4 %collective-permute-start.16 = (bf16[256,768]{1,0:T(8,128)(2,1)}, bf16[256,768]{1,0:T(8,128)(2,1)}, u32[]{:S(2)}, u32[]{:S(2)}) collective-permute-start(bf16[256,768]{1,0:T(8,128)(2,1)} %get-tuple-element.112), channel_id=1, source_target_pairs={{0,2},{2,0},{4,6},{6,4},{1,3},{3,1},{5,7},{7,5}} | collective-permute-start | bytes 1179656 | tf_op jit(solution)/shard_map/ppermute | solution.py:422
  145.1 16.2 %collective-permute-start.17 = (bf16[256,768]{1,0:T(8,128)(2,1)S(1)}, bf16[256,768]{1,0:T(8,128)(2,1)}, u32[]{:S(2)}, u32[]{:S(2)}) collective-permute-start(bf16[256,768]{1,0:T(8,128)(2,1)S(1)} %get-tuple-element.113), channel_id=1, source_target_pairs={{0,4},{2,6},{4,0},{6,2},{1,5},{3,7},{5,1},{7,3}} | collective-permute-start | bytes 1179656 | tf_op jit(solution)/shard_map/ppermute | solution.py:422
  153.6 11.9 %collective-permute-start.20 = (bf16[256,768]{1,0:T(8,128)(2,1)}, bf16[256,768]{1,0:T(8,128)(2,1)}, u32[]{:S(2)}, u32[]{:S(2)}) collective-permute-start(bf16[256,768]{1,0:T(8,128)(2,1)} %collective-permute-done.18.refs_5_), channel_id=1, source_target_pairs={{0,2},{2,0},{4,6},{6,4},{1,3},{3,1},{5,7},{7,5}} | collective-permute-start | bytes 1179656 | tf_op jit(solution)/shard_map/ppermute | solution.py:422
  155.6 9.9 %collective-permute-start.19 = (bf16[256,768]{1,0:T(8,128)(2,1)}, bf16[256,768]{1,0:T(8,128)(2,1)}, u32[]{:S(2)}, u32[]{:S(2)}) collective-permute-start(bf16[256,768]{1,0:T(8,128)(2,1)} %collective-permute-done.15.refs_2_), channel_id=1, source_target_pairs={{0,4},{2,6},{4,0},{6,2},{1,5},{3,7},{5,1},{7,3}} | collective-permute-start | bytes 1179656 | tf_op jit(solution)/shard_map/ppermute | solution.py:422
  260.8 52.5 %copy-start.13 = (bf16[512,768]{1,0:T(8,128)(2,1)S(1)}, bf16[512,768]{1,0:T(8,128)(2,1)}, u32[]{:S(2)}) copy-start(bf16[512,768]{1,0:T(8,128)(2,1)} %get-tuple-element.68) | copy-start | bytes 2359300
  260.8 59.8 %collective-permute-start.31 = (bf16[2,3,1344,768]{3,2,1,0:T(8,128)(2,1)}, bf16[2,3,1344,768]{3,2,1,0:T(8,128)(2,1)}, u32[]{:S(2)}, u32[]{:S(2)}) collective-permute-start(bf16[2,3,1344,768]{3,2,1,0:T(8,128)(2,1)} %expert_weight_grad.5.own_ref), channel_id=1, source_target_pairs={{0,1},{1,0},{2,3},{3,2},{4,5},{5,4},{6,7},{7,6}} | collective-permute-start | bytes 37158920 | tf_op jit(solution)/shard_map/ppermute | solution.py:422
  274.9 58.6 %collective-permute-start.30 = (bf16[2,3,1344,768]{3,2,1,0:T(8,128)(2,1)}, bf16[2,3,1344,768]{3,2,1,0:T(8,128)(2,1)}, u32[]{:S(2)}, u32[]{:S(2)}) collective-permute-start(bf16[2,3,1344,768]{3,2,1,0:T(8,128)(2,1)} %expert_weight_grad.4.own_ref), channel_id=1, source_target_pairs={{0,1},{1,0},{2,3},{3,2},{4,5},{5,4},{6,7},{7,6}} | collective-permute-start | bytes 37158920 | tf_op jit(solution)/shard_map/ppermute | solution.py:422
  275.3 20.6 %collective-permute-start.24 = (bf16[512,768]{1,0:T(8,128)(2,1)}, bf16[512,768]{1,0:T(8,128)(2,1)S(1)}, u32[]{:S(2)}, u32[]{:S(2)}) collective-permute-start(bf16[512,768]{1,0:T(8,128)(2,1)} %get-tuple-element.69), channel_id=1, source_target_pairs={{0,2},{2,0},{4,6},{6,4},{1,3},{3,1},{5,7},{7,5}} | collective-permute-start | bytes 2359304 | tf_op jit(solution)/shard_map/ppermute | solution.py:422
  277.0 36.4 %collective-permute-start.25 = (bf16[512,768]{1,0:T(8,128)(2,1)}, bf16[512,768]{1,0:T(8,128)(2,1)S(1)}, u32[]{:S(2)}, u32[]{:S(2)}) collective-permute-start(bf16[512,768]{1,0:T(8,128)(2,1)} %get-tuple-element.70), channel_id=1, source_target_pairs={{0,4},{2,6},{4,0},{6,2},{1,5},{3,7},{5,1},{7,3}} | collective-permute-start | bytes 2359304 | tf_op jit(solution)/shard_map/ppermute | solution.py:422
  277.0 36.4 %collective-permute-start.26 = (bf16[512,768]{1,0:T(8,128)(2,1)S(1)}, bf16[512,768]{1,0:T(8,128)(2,1)S(1)}, u32[]{:S(2)}, u32[]{:S(2)}) collective-permute-start(bf16[512,768]{1,0:T(8,128)(2,1)S(1)} %copy-done.30), channel_id=1, source_target_pairs={{0,6},{2,4},{4,2},{6,0},{1,7},{3,5},{5,3},{7,1}} | collective-permute-start | bytes 2359304 | tf_op jit(solution)/shard_map/ppermute | solution.py:422
  316.2 30.1 %collective-permute-start.29 = (bf16[512,768]{1,0:T(8,128)(2,1)S(1)}, bf16[512,768]{1,0:T(8,128)(2,1)}, u32[]{:S(2)}, u32[]{:S(2)}) collective-permute-start(bf16[512,768]{1,0:T(8,128)(2,1)S(1)} %add_convert_fusion.3.refs_8_), channel_id=1, source_target_pairs={{0,6},{2,4},{4,2},{6,0},{1,7},{3,5},{5,3},{7,1}} | collective-permute-start | bytes 2359304 | tf_op jit(solution)/shard_map/ppermute | solution.py:422
  317.4 35.4 %collective-permute-start.28 = (bf16[512,768]{1,0:T(8,128)(2,1)S(1)}, bf16[512,768]{1,0:T(8,128)(2,1)}, u32[]{:S(2)}, u32[]{:S(2)}) collective-permute-start(bf16[512,768]{1,0:T(8,128)(2,1)S(1)} %add_convert_fusion.3.refs_8_), channel_id=1, source_target_pairs={{0,4},{2,6},{4,0},{6,2},{1,5},{3,7},{5,1},{7,3}} | collective-permute-start | bytes 2359304 | tf_op jit(solution)/shard_map/ppermute | solution.py:422
  318.0 34.8 %collective-permute-start.27 = (bf16[512,768]{1,0:T(8,128)(2,1)S(1)}, bf16[512,768]{1,0:T(8,128)(2,1)}, u32[]{:S(2)}, u32[]{:S(2)}) collective-permute-start(bf16[512,768]{1,0:T(8,128)(2,1)S(1)} %add_convert_fusion.3.refs_8_), channel_id=1, source_target_pairs={{0,2},{2,0},{4,6},{6,4},{1,3},{3,1},{5,7},{7,5}} | collective-permute-start | bytes 2359304 | tf_op jit(solution)/shard_map/ppermute | solution.py:422
  430.3 25.9 %copy-start.10 = (bf16[512,768]{1,0:T(8,128)(2,1)S(1)}, bf16[512,768]{1,0:T(8,128)(2,1)}, u32[]{:S(2)}) copy-start(bf16[512,768]{1,0:T(8,128)(2,1)} %copy-done.9) | copy-start | bytes 2359300
  430.3 25.9 %copy-start.17 = (bf16[256,768]{1,0:T(8,128)(2,1)S(1)}, bf16[256,768]{1,0:T(8,128)(2,1)}, u32[]{:S(2)}) copy-start(bf16[256,768]{1,0:T(8,128)(2,1)} %copy-done.16) | copy-start | bytes 1179652
  430.3 25.9 %copy-start.19 = (bf16[256,768]{1,0:T(8,128)(2,1)S(1)}, bf16[256,768]{1,0:T(8,128)(2,1)}, u32[]{:S(2)}) copy-start(bf16[256,768]{1,0:T(8,128)(2,1)} %copy-done.18) | copy-start | bytes 1179652
  430.3 158.0 %collective-permute-start.55 = (bf16[2,3,1344,768]{3,2,1,0:T(8,128)(2,1)}, bf16[2,3,1344,768]{3,2,1,0:T(8,128)(2,1)}, u32[]{:S(2)}, u32[]{:S(2)}) collective-permute-start(bf16[2,3,1344,768]{3,2,1,0:T(8,128)(2,1)} %expert_weight_grad.7.own_ref), channel_id=1, source_target_pairs={{0,1},{1,0},{2,3},{3,2},{4,5},{5,4},{6,7},{7,6}} | collective-permute-start | bytes 37158920 | tf_op jit(solution)/shard_map/ppermute | solution.py:422
  455.8 145.3 %collective-permute-start.54 = (bf16[2,3,1344,768]{3,2,1,0:T(8,128)(2,1)}, bf16[2,3,1344,768]{3,2,1,0:T(8,128)(2,1)}, u32[]{:S(2)}, u32[]{:S(2)}) collective-permute-start(bf16[2,3,1344,768]{3,2,1,0:T(8,128)(2,1)} %expert_weight_grad.6.own_ref), channel_id=1, source_target_pairs={{0,1},{1,0},{2,3},{3,2},{4,5},{5,4},{6,7},{7,6}} | collective-permute-start | bytes 37158920 | tf_op jit(solution)/shard_map/ppermute | solution.py:422
  457.0 18.7 %collective-permute-start.46 = (bf16[384,768]{1,0:T(8,128)(2,1)S(1)}, bf16[384,768]{1,0:T(8,128)(2,1)S(1)}, u32[]{:S(2)}, u32[]{:S(2)}) collective-permute-start(bf16[384,768]{1,0:T(8,128)(2,1)S(1)} %constant_dynamic-slice_fusion.3), channel_id=1, source_target_pairs={{0,1},{1,0},{2,3},{3,2},{4,5},{5,4},{6,7},{7,6}} | collective-permute-start | bytes 1769480 | tf_op jit(solution)/shard_map/ppermute | solution.py:422
  457.2 25.1 %collective-permute-start.35 = (bf16[512,768]{1,0:T(8,128)(2,1)}, bf16[512,768]{1,0:T(8,128)(2,1)S(1)}, u32[]{:S(2)}, u32[]{:S(2)}) collective-permute-start(bf16[512,768]{1,0:T(8,128)(2,1)} %get-tuple-element.92), channel_id=1, source_target_pairs={{0,2},{2,0},{4,6},{6,4},{1,3},{3,1},{5,7},{7,5}} | collective-permute-start | bytes 2359304 | tf_op jit(solution)/shard_map/ppermute | solution.py:422
  457.2 25.1 %collective-permute-start.36 = (bf16[512,768]{1,0:T(8,128)(2,1)}, bf16[512,768]{1,0:T(8,128)(2,1)S(1)}, u32[]{:S(2)}, u32[]{:S(2)}) collective-permute-start(bf16[512,768]{1,0:T(8,128)(2,1)} %get-tuple-element.93), channel_id=1, source_target_pairs={{0,4},{2,6},{4,0},{6,2},{1,5},{3,7},{5,1},{7,3}} | collective-permute-start | bytes 2359304 | tf_op jit(solution)/shard_map/ppermute | solution.py:422
  476.6 22.5 %collective-permute-start.37 = (bf16[512,768]{1,0:T(8,128)(2,1)}, bf16[512,768]{1,0:T(8,128)(2,1)}, u32[]{:S(2)}, u32[]{:S(2)}) collective-permute-start(bf16[512,768]{1,0:T(8,128)(2,1)} %get-tuple-element.94), channel_id=1, source_target_pairs={{0,6},{2,4},{4,2},{6,0},{1,7},{3,5},{5,3},{7,1}} | collective-permute-start | bytes 2359304 | tf_op jit(solution)/shard_map/ppermute | solution.py:422
  482.3 23.3 %collective-permute-start.47 = (bf16[96,768]{1,0:T(8,128)(2,1)S(1)}, bf16[96,768]{1,0:T(8,128)(2,1)S(1)}, u32[]{:S(2)}, u32[]{:S(2)}) collective-permute-start(bf16[96,768]{1,0:T(8,128)(2,1)S(1)} %get-tuple-element.119), channel_id=1, source_target_pairs={{0,2},{2,0},{4,6},{6,4},{1,3},{3,1},{5,7},{7,5}} | collective-permute-start | bytes 442376 | tf_op jit(solution)/shard_map/ppermute | solution.py:422
  502.6 13.7 %collective-permute-start.38 = (bf16[384,768]{1,0:T(8,128)(2,1)S(1)}, bf16[384,768]{1,0:T(8,128)(2,1)}, u32[]{:S(2)}, u32[]{:S(2)}) collective-permute-start(bf16[384,768]{1,0:T(8,128)(2,1)S(1)} %dynamic-slice_bitcast_fusion), channel_id=1, source_target_pairs={{0,1},{1,0},{2,3},{3,2},{4,5},{5,4},{6,7},{7,6}} | collective-permute-start | bytes 1769480 | tf_op jit(solution)/shard_map/ppermute | solution.py:422
  502.6 7.7 %collective-permute-start.49 = (bf16[96,768]{1,0:T(8,128)(2,1)}, bf16[96,768]{1,0:T(8,128)(2,1)S(1)}, u32[]{:S(2)}, u32[]{:S(2)}) collective-permute-start(bf16[96,768]{1,0:T(8,128)(2,1)} %get-tuple-element.120), channel_id=1, source_target_pairs={{0,6},{2,4},{4,2},{6,0},{1,7},{3,5},{5,3},{7,1}} | collective-permute-start | bytes 442376 | tf_op jit(solution)/shard_map/ppermute | solution.py:422
  505.6 8.0 %collective-permute-start.48 = (bf16[96,768]{1,0:T(8,128)(2,1)}, bf16[96,768]{1,0:T(8,128)(2,1)}, u32[]{:S(2)}, u32[]{:S(2)}) collective-permute-start(bf16[96,768]{1,0:T(8,128)(2,1)} %get-tuple-element.121), channel_id=1, source_target_pairs={{0,4},{2,6},{4,0},{6,2},{1,5},{3,7},{5,1},{7,3}} | collective-permute-start | bytes 442376 | tf_op jit(solution)/shard_map/ppermute | solution.py:422
  514.5 7.7 %collective-permute-start.52 = (bf16[96,768]{1,0:T(8,128)(2,1)S(1)}, bf16[96,768]{1,0:T(8,128)(2,1)S(1)}, u32[]{:S(2)}, u32[]{:S(2)}) collective-permute-start(bf16[96,768]{1,0:T(8,128)(2,1)S(1)} %add_convert_fusion.12), channel_id=1, source_target_pairs={{0,6},{2,4},{4,2},{6,0},{1,7},{3,5},{5,3},{7,1}} | collective-permute-start | bytes 442376 | tf_op jit(solution)/shard_map/ppermute | solution.py:422
  516.3 8.1 %collective-permute-start.51 = (bf16[96,768]{1,0:T(8,128)(2,1)S(1)}, bf16[96,768]{1,0:T(8,128)(2,1)S(1)}, u32[]{:S(2)}, u32[]{:S(2)}) collective-permute-start(bf16[96,768]{1,0:T(8,128)(2,1)S(1)} %add_convert_fusion.12), channel_id=1, source_target_pairs={{0,4},{2,6},{4,0},{6,2},{1,5},{3,7},{5,1},{7,3}} | collective-permute-start | bytes 442376 | tf_op jit(solution)/shard_map/ppermute | solution.py:422
  516.3 8.1 %collective-permute-start.50 = (bf16[96,768]{1,0:T(8,128)(2,1)S(1)}, bf16[96,768]{1,0:T(8,128)(2,1)S(1)}, u32[]{:S(2)}, u32[]{:S(2)}) collective-permute-start(bf16[96,768]{1,0:T(8,128)(2,1)S(1)} %add_convert_fusion.12), channel_id=1, source_target_pairs={{0,2},{2,0},{4,6},{6,4},{1,3},{3,1},{5,7},{7,5}} | collective-permute-start | bytes 442376 | tf_op jit(solution)/shard_map/ppermute | solution.py:422
  522.2 5.4 collective-permute-start.39
  525.1 13.7 %collective-permute-start.53 = (bf16[384,768]{1,0:T(8,128)(2,1)S(1)}, bf16[384,768]{1,0:T(8,128)(2,1)S(1)}, u32[]{:S(2)}, u32[]{:S(2)}) collective-permute-start(bf16[384,768]{1,0:T(8,128)(2,1)S(1)} %bitcast.95), channel_id=1, source_target_pairs={{0,1},{1,0},{2,3},{3,2},{4,5},{5,4},{6,7},{7,6}} | collective-permute-start | bytes 1769480 | tf_op jit(solution)/shard_map/ppermute | solution.py:422
  525.1 7.5 %collective-permute-start.41 = (bf16[96,768]{1,0:T(8,128)(2,1)}, bf16[96,768]{1,0:T(8,128)(2,1)S(1)}, u32[]{:S(2)}, u32[]{:S(2)}) collective-permute-start(bf16[96,768]{1,0:T(8,128)(2,1)} %get-tuple-element.117), channel_id=1, source_target_pairs={{0,6},{2,4},{4,2},{6,0},{1,7},{3,5},{5,3},{7,1}} | collective-permute-start | bytes 442376 | tf_op jit(solution)/shard_map/ppermute | solution.py:422
  527.6 8.0 %collective-permute-start.40 = (bf16[96,768]{1,0:T(8,128)(2,1)S(1)}, bf16[96,768]{1,0:T(8,128)(2,1)S(1)}, u32[]{:S(2)}, u32[]{:S(2)}) collective-permute-start(bf16[96,768]{1,0:T(8,128)(2,1)S(1)} %get-tuple-element.118), channel_id=1, source_target_pairs={{0,4},{2,6},{4,0},{6,2},{1,5},{3,7},{5,1},{7,3}} | collective-permute-start | bytes 442376 | tf_op jit(solution)/shard_map/ppermute | solution.py:422
  535.7 7.6 %collective-permute-start.44 = (bf16[96,768]{1,0:T(8,128)(2,1)S(1)}, bf16[96,768]{1,0:T(8,128)(2,1)S(1)}, u32[]{:S(2)}, u32[]{:S(2)}) collective-permute-start(bf16[96,768]{1,0:T(8,128)(2,1)S(1)} %add_convert_fusion.13), channel_id=1, source_target_pairs={{0,6},{2,4},{4,2},{6,0},{1,7},{3,5},{5,3},{7,1}} | collective-permute-start | bytes 442376 | tf_op jit(solution)/shard_map/ppermute | solution.py:422
  537.0 29.3 %collective-permute-start.32 = (bf16[512,768]{1,0:T(8,128)(2,1)}, bf16[512,768]{1,0:T(8,128)(2,1)}, u32[]{:S(2)}, u32[]{:S(2)}) collective-permute-start(bf16[512,768]{1,0:T(8,128)(2,1)} %get-tuple-element.85), channel_id=1, source_target_pairs={{0,2},{2,0},{4,6},{6,4},{1,3},{3,1},{5,7},{7,5}} | collective-permute-start | bytes 2359304 | tf_op jit(solution)/shard_map/ppermute | solution.py:422
  538.7 6.8 %collective-permute-start.43 = (bf16[96,768]{1,0:T(8,128)(2,1)S(1)}, bf16[96,768]{1,0:T(8,128)(2,1)S(1)}, u32[]{:S(2)}, u32[]{:S(2)}) collective-permute-start(bf16[96,768]{1,0:T(8,128)(2,1)S(1)} %add_convert_fusion.13), channel_id=1, source_target_pairs={{0,4},{2,6},{4,0},{6,2},{1,5},{3,7},{5,1},{7,3}} | collective-permute-start | bytes 442376 | tf_op jit(solution)/shard_map/ppermute | solution.py:422
  543.3 19.2 %collective-permute-start.42 = (bf16[96,768]{1,0:T(8,128)(2,1)S(1)}, bf16[96,768]{1,0:T(8,128)(2,1)S(1)}, u32[]{:S(2)}, u32[]{:S(2)}) collective-permute-start(bf16[96,768]{1,0:T(8,128)(2,1)S(1)} %add_convert_fusion.13), channel_id=1, source_target_pairs={{0,2},{2,0},{4,6},{6,4},{1,3},{3,1},{5,7},{7,5}} | collective-permute-start | bytes 442376 | tf_op jit(solution)/shard_map/ppermute | solution.py:422
  545.5 35.9 %collective-permute-start.33 = (bf16[512,768]{1,0:T(8,128)(2,1)}, bf16[512,768]{1,0:T(8,128)(2,1)}, u32[]{:S(2)}, u32[]{:S(2)}) collective-permute-start(bf16[512,768]{1,0:T(8,128)(2,1)} %get-tuple-element.86), channel_id=1, source_target_pairs={{0,4},{2,6},{4,0},{6,2},{1,5},{3,7},{5,1},{7,3}} | collective-permute-start | bytes 2359304 | tf_op jit(solution)/shard_map/ppermute | solution.py:422
  563.2 19.9 %collective-permute-start.34 = (bf16[512,768]{1,0:T(8,128)(2,1)}, bf16[512,768]{1,0:T(8,128)(2,1)}, u32[]{:S(2)}, u32[]{:S(2)}) collective-permute-start(bf16[512,768]{1,0:T(8,128)(2,1)} %get-tuple-element.87), channel_id=1, source_target_pairs={{0,6},{2,4},{4,2},{6,0},{1,7},{3,5},{5,3},{7,1}} | collective-permute-start | bytes 2359304 | tf_op jit(solution)/shard_map/ppermute | solution.py:422
  566.4 19.8 %collective-permute-start.45 = (bf16[384,768]{1,0:T(8,128)(2,1)S(1)}, bf16[384,768]{1,0:T(8,128)(2,1)S(1)}, u32[]{:S(2)}, u32[]{:S(2)}) collective-permute-start(bf16[384,768]{1,0:T(8,128)(2,1)S(1)} %bitcast.97), channel_id=1, source_target_pairs={{0,1},{1,0},{2,3},{3,2},{4,5},{5,4},{6,7},{7,6}} | collective-permute-start | bytes 1769480 | tf_op jit(solution)/shard_map/ppermute | solution.py:422
  (23 other events, 205.3 us)
